TPU v7x, 16 devices: a 4x2x1 block of a 4x4x8 slice. The times are simulated.
16 devices in a mesh: dp: 2 (over y, z), ep: 8 (over x, core).
Axes of the slice: x: 4, y: 2, z: 1, core: 2. Of those that a mesh axis runs over, the one named last changes fastest.
The devices are a block of a 4x4x8 slice.
Arguments:
- x_in: bfloat16 [256, 512, 768], P(('dp', 'ep')), parts along dimension 0
- pad_mask: int32 [256, 512], P(('dp', 'ep')), parts along dimension 0
- rel_bias: float32 [12, 512, 512], replicated
- expert_idx: int32 [2, 256, 512], P(None, ('dp', 'ep')), parts along dimension 1
- norm_scale: float32 [2, 2, 768], replicated
- w_query: bfloat16 [2, 768, 768], replicated
- w_key: bfloat16 [2, 768, 768], replicated
- w_value: bfloat16 [2, 768, 768], replicated
- w_attn_out: bfloat16 [2, 768, 768], replicated
- w_router: float32 [2, 768, 16], replicated
- w_in: bfloat16 [2, 16, 768, 3072], P(None, 'ep')
- w_out: bfloat16 [2, 16, 3072, 768], P(None, 'ep')
Outputs:
- output: bfloat16 [256, 512, 768], P(('dp', 'ep')), parts along dimension 0
There are 2 independent parts. A program takes and returns all parts, laid end to end along the dimension named above; an argument that names none is the same for every part.
All inputs are finite; a program needn't handle non-finite values.
Results may differ from a plain program's by a relative error of at most 0.0189939.
Values are sent between devices in bfloat16 or wider.
A program may use at most 768 MiB of HBM per device.

v0:
```python
import jax
import jax.numpy as jnp
from jax import lax
from jax.sharding import PartitionSpec as P, NamedSharding

NORM_EPS = 1e-6
NEG_BIG = -1e9
CAP_FACTOR = 2


def rms_norm(hidden, gain):
    hid32 = hidden.astype(jnp.float32)
    return hid32 * lax.rsqrt(jnp.mean(hid32 * hid32, axis=-1, keepdims=True) + NORM_EPS) * gain


def attention(hidden, pad_mask, rel_bias, gain, query_w, key_w, value_w, out_w):
    num_seqs, seq_len, model_dim = hidden.shape
    num_heads = rel_bias.shape[0]
    head_dim = query_w.shape[1] // num_heads
    normed = rms_norm(hidden, gain).astype(jnp.bfloat16)

    def project(weight):
        out_rows = jnp.einsum('std,de->ste', normed, weight, preferred_element_type=jnp.float32)
        return out_rows.astype(jnp.bfloat16).reshape(num_seqs, seq_len, num_heads, head_dim)

    query_rows = project(query_w)
    key_rows = project(key_w)
    value_rows = project(value_w)
    scores = jnp.einsum('sqhd,skhd->shqk', query_rows, key_rows, preferred_element_type=jnp.float32)
    scores = scores + rel_bias[None] + jnp.where(pad_mask > 0, 0.0, NEG_BIG)[:, None, None, :]
    attn_probs = jax.nn.softmax(scores, axis=-1).astype(jnp.bfloat16)
    context = jnp.einsum('shqk,skhd->sqhd', attn_probs, value_rows, preferred_element_type=jnp.float32)
    context = context.astype(jnp.bfloat16).reshape(num_seqs, seq_len, num_heads * head_dim)
    attn_out = jnp.einsum('ste,ed->std', context, out_w, preferred_element_type=jnp.float32)
    return (hidden.astype(jnp.float32) + attn_out).astype(jnp.bfloat16)


def token_slots(expert_ids, num_experts):
    tok_count = expert_ids.shape[0]
    sort_order = jnp.argsort(expert_ids, stable=True)
    counts = jnp.zeros((num_experts,), jnp.int32).at[expert_ids].add(1)
    starts = jnp.cumsum(counts) - counts
    rank_sorted = jnp.arange(tok_count, dtype=jnp.int32) - starts[expert_ids[sort_order]]
    return jnp.zeros((tok_count,), jnp.int32).at[sort_order].set(rank_sorted)


def dispatch(flat_hidden, expert_ids, gain, route_w, capacity):
    tok_count, model_dim = flat_hidden.shape
    num_experts = route_w.shape[1]
    normed32 = rms_norm(flat_hidden, gain)
    logits = jnp.dot(normed32, route_w, precision=lax.Precision.HIGHEST, preferred_element_type=jnp.float32)
    gate_val = jnp.take_along_axis(jax.nn.softmax(logits, axis=-1), expert_ids[:, None], axis=1)[:, 0]
    token_slot = token_slots(expert_ids, num_experts)
    flat_slot = jnp.where(token_slot < capacity, expert_ids * capacity + token_slot, num_experts * capacity)
    slot_token = jnp.full((num_experts * capacity,), tok_count, jnp.int32).at[flat_slot].set(jnp.arange(tok_count, dtype=jnp.int32), mode='drop')
    packed = jnp.take(normed32.astype(jnp.bfloat16), slot_token, axis=0, mode='fill', fill_value=0)
    return packed.reshape(num_experts, capacity, model_dim), gate_val, flat_slot


def expert_ffn(rows_in, up_w, down_w):
    inner_act = jnp.einsum('ecd,edf->ecf', rows_in, up_w, preferred_element_type=jnp.float32)
    inner_act = jnp.maximum(inner_act, 0.0).astype(jnp.bfloat16)
    return jnp.einsum('ecf,efd->ecd', inner_act, down_w, preferred_element_type=jnp.float32).astype(jnp.bfloat16)


def combine(flat_hidden, expert_rows, gate_val, flat_slot):
    returned = jnp.take(expert_rows, flat_slot, axis=0, mode='fill', fill_value=0)
    return (flat_hidden.astype(jnp.float32) + gate_val[:, None] * returned.astype(jnp.float32)).astype(jnp.bfloat16)


def solution(mesh):
    token_spec = P(('dp', 'ep'))

    def per_device(x_in, pad_mask, rel_bias, expert_idx, norm_scale, w_query, w_key, w_value, w_attn_out, w_router, w_in, w_out):
        num_seqs, seq_len, model_dim = x_in.shape
        tok_count = num_seqs * seq_len
        num_experts = w_router.shape[2]
        capacity = (CAP_FACTOR * tok_count + num_experts - 1) // num_experts
        hidden = x_in
        for layer_id in range(w_router.shape[0]):
            hidden = attention(hidden, pad_mask, rel_bias, norm_scale[layer_id, 0], w_query[layer_id], w_key[layer_id], w_value[layer_id], w_attn_out[layer_id])
            flat_hidden = hidden.reshape(tok_count, model_dim)
            packed, gate_val, flat_slot = dispatch(flat_hidden, expert_idx[layer_id].reshape(tok_count), norm_scale[layer_id, 1], w_router[layer_id], capacity)
            received = lax.all_to_all(packed, 'ep', 0, 1, tiled=True)
            expert_rows = expert_ffn(received, w_in[layer_id], w_out[layer_id])
            returned = lax.all_to_all(expert_rows, 'ep', 1, 0, tiled=True)
            hidden = combine(flat_hidden, returned.reshape(num_experts * capacity, model_dim), gate_val, flat_slot).reshape(num_seqs, seq_len, model_dim)
        return hidden

    return jax.shard_map(per_device, mesh=mesh, in_specs=(token_spec, token_spec, P(), P(None, ('dp', 'ep')), P(), P(), P(), P(), P(), P(), P(None, 'ep'), P(None, 'ep')), out_specs=token_spec, check_vma=False)
```

profile of v0, /device:TPU:113, one launch (start us, length us, event | category | flops | bytes accessed | tf_op | source)
XLA Modules:
  0.0 2793.1 jit_solution(3956447119429446227)
XLA Ops:
  1.5 57.0 %scatter_custom_fusion = s32[16]{0:T(128)S(1)} fusion(s32[8192]{0:T(1024)S(1)} %bitcast.263, s32[8192]{0:T(1024)S(1)} %broadcast.304, s32[]{:T(128)} %constant.38.clone.1), kind=kCustom, calls=%fused_computation.208 | custom fusion | flops 8192 | bytes 68 | tf_op jit(solution)/shard_map/scatter-add | solution.py:41
  66.3 45.5 %gather_fusion = s32[8192]{0:T(1024)S(1)} fusion(s32[8192]{0:T(1024)S(1)} %bitcast.223, s32[8192]{0:T(1024)S(1)} %get-tuple-element.56), kind=kCustom, calls=%fused_computation.6 | custom fusion | bytes 98304 | tf_op jit(solution)/shard_map/gather | solution.py:43
  123.0 30.5 %scatter_custom_fusion.1 = s32[8192]{0:T(1024)S(1)} fusion(s32[8192]{0:T(1024)S(1)} %get-tuple-element.57, s32[8192]{0:T(1024)S(1)} %select_subtract_fusion.1, s32[]{:T(128)} %constant.38.clone.1), kind=kCustom, calls=%fused_computation.200 | custom fusion | bytes 32772 | tf_op jit(solution)/shard_map/scatter | solution.py:44
  305.4 98.1 %fusion.105 = (f32[16,12,512]{2,1,0:T(8,128)S(1)}, f32[16,12,512,512]{2,3,1,0:T(8,128)}) fusion(f32[16,512]{1,0:T(8,128)S(1)} %compare_select_fusion.22, f32[12,512,512]{1,2,0:T(8,128)} %copy.63, bf16[16,512,12,64]{1,3,2,0:T(8,128)(2,1)} %bitcast.231, bf16[16,512,12,64]{1,3,2,0:T(8,128)(2,1)} %bitcast.232), kind=kOutput, calls=%fused_computation.216 | convolution fusion | flops 6643778048 | bytes 239501312 | tf_op jit(solution)/shard_map/sub | solution.py:31
  403.5 69.1 %fusion.46 = bf16[16,12,64,512]{3,2,1,0:T(8,128)(2,1)} fusion(bf16[16,512,12,64]{1,3,2,0:T(8,128)(2,1)} %bitcast.243, f32[16,12,512,512]{2,3,1,0:T(8,128)} %get-tuple-element.91, f32[16,12,512]{2,1,0:T(8,128)S(1)} %get-tuple-element.90), kind=kOutput, calls=%fused_computation.88 | convolution fusion | flops 6549405696 | bytes 226885632 | tf_op jit(solution)/shard_map/shqk,skhd->sqhd/dot_general | solution.py:32
  507.5 79.3 %gather_fusion.3 = bf16[16384,768]{1,0:T(8,128)(2,1)} fusion(bf16[8192,768]{1,0:T(8,128)(2,1)} %fusion.30, s32[16384]{0:T(1024)S(1)} %copy-done.9), kind=kCustom, calls=%fused_computation.1.clone | custom fusion | bytes 50397184 | tf_op jit(solution)/shard_map/jit(_take)/gather | solution.py:56
  602.1 279.5 %all_to_all.66 = bf16[16,1024,768]{2,1,0:T(8,128)(2,1)} all-to-all(bf16[16,1024,768]{2,1,0:T(8,128)(2,1)S(1)} %bitcast.235), channel_id=1, replica_groups=mesh['dp'=2,'ep'=8] {'ep'}, dimensions={0} | all-to-all | bytes 50331648 | tf_op jit(solution)/shard_map/all_to_all | solution.py:84
  902.4 87.5 %fusion.39 = bf16[2,8192,3072]{2,1,0:T(8,128)(2,1)} fusion(bf16[2,8192,768]{2,1,0:T(8,128)(2,1)} %bitcast.240, bf16[2,2,768,3072]{3,2,1,0:T(8,128)(2,1)} %param.28), kind=kOutput, calls=%fused_computation.75 | convolution fusion | flops 77309411328 | bytes 135266304 | tf_op jit(solution)/shard_map/ecd,edf->ecf/dot_general | solution.py:61
  990.0 88.4 %fusion.33 = bf16[2,8192,768]{2,1,0:T(8,128)(2,1)} fusion(bf16[2,8192,3072]{2,1,0:T(8,128)(2,1)} %fusion.39, bf16[2,2,3072,768]{3,2,1,0:T(8,128)(2,1)} %param.29), kind=kOutput, calls=%fused_computation.69 | convolution fusion | flops 77472989184 | bytes 135266304 | tf_op jit(solution)/shard_map/ecf,efd->ecd/dot_general | solution.py:63
  1078.4 45.8 %copy.68 = bf16[2,8192,768]{2,0,1:T(2,128)(2,1)} copy(bf16[2,8192,768]{2,1,0:T(8,128)(2,1)} %fusion.33) | data formatting | bytes 50331648 | tf_op jit(solution)/shard_map/convert_element_type | solution.py:63
  1131.8 57.2 %scatter_custom_fusion.3 = s32[16]{0:T(128)S(1)} fusion(s32[8192]{0:T(1024)S(1)} %bitcast.264, s32[8192]{0:T(1024)} %copy-done.28, s32[]{:T(128)} %constant.38.clone.1), kind=kCustom, calls=%fused_computation.206 | custom fusion | flops 8192 | bytes 576 | tf_op jit(solution)/shard_map/scatter-add | solution.py:41
  1196.1 45.7 %gather_fusion.1 = s32[8192]{0:T(1024)S(1)} fusion(s32[8192]{0:T(1024)S(1)} %bitcast.220, s32[8192]{0:T(1024)S(1)} %get-tuple-element.52), kind=kCustom, calls=%fused_computation.7 | custom fusion | bytes 98304 | tf_op jit(solution)/shard_map/gather | solution.py:43
  1281.8 65.5 %gather_fusion.2 = f32[8192]{0:T(1024)S(1)} fusion(f32[8192,16]{0,1:T(8,128)S(1)} %fusion.66, s32[8192]{0:T(1024)S(1)} %bitcast.228), kind=kCustom, calls=%fused_computation.clone | custom fusion | bytes 131072 | tf_op jit(solution)/shard_map/jit(take_along_axis)/gather | solution.py:52
  1444.9 48.4 %gather_fusion.4 = bf16[8192,768]{1,0:T(8,128)(2,1)} fusion(bf16[16384,768]{1,0:T(8,128)(2,1)} %bitcast.225, s32[8192]{0:T(1024)S(1)} %broadcast_clamp_fusion.1), kind=kCustom, calls=%fused_computation.2.clone | custom fusion | bytes 25198592 | tf_op jit(solution)/shard_map/jit(_take)/gather | solution.py:67
  1605.5 98.1 %fusion.107 = (f32[16,12,512]{2,1,0:T(8,128)S(1)}, f32[16,12,512,512]{2,3,1,0:T(8,128)}) fusion(f32[16,512]{1,0:T(8,128)S(1)} %copy-done.3, f32[12,512,512]{1,2,0:T(8,128)} %copy.63, bf16[16,512,12,64]{1,3,2,0:T(8,128)(2,1)} %bitcast.233, bf16[16,512,12,64]{1,3,2,0:T(8,128)(2,1)} %bitcast.234), kind=kOutput, calls=%fused_computation.218 | convolution fusion | flops 6643778048 | bytes 239501312 | tf_op jit(solution)/shard_map/sub | solution.py:31
  1703.5 69.1 %fusion.45 = bf16[16,12,64,512]{3,2,1,0:T(8,128)(2,1)} fusion(bf16[16,512,12,64]{1,3,2,0:T(8,128)(2,1)} %bitcast.242, f32[16,12,512,512]{2,3,1,0:T(8,128)} %get-tuple-element.97, f32[16,12,512]{2,1,0:T(8,128)S(1)} %get-tuple-element.96), kind=kOutput, calls=%fused_computation.87 | convolution fusion | flops 6549405696 | bytes 226885632 | tf_op jit(solution)/shard_map/shqk,skhd->sqhd/dot_general | solution.py:32
  1808.8 79.3 %gather_fusion.6 = bf16[16384,768]{1,0:T(8,128)(2,1)} fusion(bf16[8192,768]{1,0:T(8,128)(2,1)} %fusion.25, s32[16384]{0:T(1024)S(1)} %copy-done.8), kind=kCustom, calls=%fused_computation.4.clone | custom fusion | bytes 50397184 | tf_op jit(solution)/shard_map/jit(_take)/gather | solution.py:56
  1903.3 278.4 %all_to_all.67 = bf16[16,1024,768]{2,1,0:T(8,128)(2,1)} all-to-all(bf16[16,1024,768]{2,1,0:T(8,128)(2,1)S(1)} %bitcast.236), channel_id=1, replica_groups=mesh['dp'=2,'ep'=8] {'ep'}, dimensions={0} | all-to-all | bytes 50331648 | tf_op jit(solution)/shard_map/all_to_all | solution.py:84
  2202.5 87.5 %fusion.36 = bf16[2,8192,3072]{2,1,0:T(8,128)(2,1)} fusion(bf16[2,8192,768]{2,1,0:T(8,128)(2,1)} %bitcast.241, bf16[2,2,768,3072]{3,2,1,0:T(8,128)(2,1)} %param.28), kind=kOutput, calls=%fused_computation.72 | convolution fusion | flops 77309411328 | bytes 135266304 | tf_op jit(solution)/shard_map/ecd,edf->ecf/dot_general | solution.py:61
  2290.1 88.3 %fusion.32 = bf16[2,8192,768]{2,1,0:T(8,128)(2,1)} fusion(bf16[2,8192,3072]{2,1,0:T(8,128)(2,1)} %fusion.36, bf16[2,2,3072,768]{3,2,1,0:T(8,128)(2,1)} %param.29), kind=kOutput, calls=%fused_computation.68 | convolution fusion | flops 77472989184 | bytes 135266304 | tf_op jit(solution)/shard_map/ecf,efd->ecd/dot_general | solution.py:63
  2378.4 45.8 %copy.77 = bf16[2,8192,768]{2,0,1:T(2,128)(2,1)} copy(bf16[2,8192,768]{2,1,0:T(8,128)(2,1)} %fusion.32) | data formatting | bytes 50331648 | tf_op jit(solution)/shard_map/convert_element_type | solution.py:63
  2471.2 65.5 %gather_fusion.5 = f32[8192]{0:T(1024)S(1)} fusion(f32[8192,16]{0,1:T(8,128)S(1)} %fusion.68, s32[8192]{0:T(1024)S(1)} %bitcast.227), kind=kCustom, calls=%fused_computation.3.clone | custom fusion | bytes 131072 | tf_op jit(solution)/shard_map/jit(take_along_axis)/gather | solution.py:52
  2536.8 168.6 %all-to-all-done.3 = bf16[2,8192,768]{2,0,1:T(2,128)(2,1)} async-done(((bf16[2,8192,768]{2,0,1:T(2,128)(2,1)}), bf16[2,8192,768]{2,0,1:T(2,128)(2,1)}, u32[]{:S(2)}, u32[]{:S(2)}) %all-to-all-start.3) | async-done | bytes 25165856 | tf_op jit(solution)/shard_map/all_to_all | solution.py:86
  2728.3 48.4 %gather_fusion.7 = bf16[8192,768]{1,0:T(8,128)(2,1)} fusion(bf16[16384,768]{1,0:T(8,128)(2,1)} %bitcast.226, s32[8192]{0:T(1024)S(1)} %broadcast_clamp_fusion), kind=kCustom, calls=%fused_computation.5.clone | custom fusion | bytes 25198592 | tf_op jit(solution)/shard_map/jit(_take)/gather | solution.py:67
  (170 shorter events, 665.1 us)
Async XLA Ops:
  1.4 58.0 %copy-start.4 = (s32[1,1,16,512]{3,1,2,0:T(1,128)}, s32[1,1,16,512]{3,1,2,0:T(1,128)S(1)}, u32[]{:S(2)}) copy-start(s32[1,1,16,512]{3,1,2,0:T(1,128)S(1)} %copy.83) | copy-start | bytes 98308
  1.5 64.8 %copy-start.28 = (s32[8192]{0:T(1024)}, s32[8192]{0:T(1024)S(1)}, u32[]{:S(2)}) copy-start(s32[8192]{0:T(1024)S(1)} %broadcast.304) | copy-start | bytes 98308
  66.3 119.5 %copy-start.31 = (f32[2,2,768]{2,1,0:T(2,128)S(1)}, f32[2,2,768]{2,1,0:T(2,128)}, u32[]{:S(2)}) copy-start(f32[2,2,768]{2,1,0:T(2,128)} %param.22) | copy-start | bytes 36868
  111.9 81.8 %copy-start.32 = (bf16[2,768,768]{2,1,0:T(8,128)(2,1)S(1)}, bf16[2,768,768]{2,1,0:T(8,128)(2,1)}, u32[]{:S(2)}) copy-start(bf16[2,768,768]{2,1,0:T(8,128)(2,1)} %param.23) | copy-start | bytes 7077892
  154.1 55.9 %copy-start.10 = (s32[8192]{0:T(1024)}, s32[8192]{0:T(1024)S(1)}, u32[]{:S(2)}) copy-start(s32[8192]{0:T(1024)S(1)} %get-tuple-element.41) | copy-start | bytes 98308
  272.2 33.2 %copy-start.2 = (f32[16,512]{1,0:T(8,128)}, f32[16,512]{1,0:T(8,128)S(1)}, u32[]{:S(2)}) copy-start(f32[16,512]{1,0:T(8,128)S(1)} %compare_select_fusion.22) | copy-start | bytes 98308
  403.5 69.1 %copy-start.35 = (bf16[2,768,768]{2,1,0:T(8,128)(2,1)S(1)}, bf16[2,768,768]{2,1,0:T(8,128)(2,1)}, u32[]{:S(2)}) copy-start(bf16[2,768,768]{2,1,0:T(8,128)(2,1)} %param.26) | copy-start | bytes 7077892
  507.5 79.3 %copy-start.21 = (pred[16384]{0:T(1024)(128)(4,1)S(1)}, pred[16384]{0:T(1024)(128)(4,1)}, u32[]{:S(2)}) copy-start(pred[16384]{0:T(1024)(128)(4,1)} %compare_and_fusion.1) | copy-start | bytes 49156
  1124.2 65.1 %copy-start.14 = (s32[2,4,8,128]{3,2,1,0:T(8,128)S(1)}, s32[2,4,8,128]{3,2,1,0:T(8,128)}, u32[]{:S(2)}) copy-start(s32[2,4,8,128]{3,2,1,0:T(8,128)} %get-tuple-element.46) | copy-start | bytes 98308
  1124.2 297.6 %all-to-all-start.1 = ((bf16[2,8192,768]{2,0,1:T(2,128)(2,1)}), bf16[2,8192,768]{2,0,1:T(2,128)(2,1)}, u32[]{:S(2)}, u32[]{:S(2)}) async-start(bf16[2,8192,768]{2,0,1:T(2,128)(2,1)} %copy.68), calls=%async_computation.1 | async-start | bytes 50331648 | tf_op jit(solution)/shard_map/all_to_all | solution.py:86
  1131.8 149.0 %copy-start.6 = (s32[1,1,16,512]{3,1,2,0:T(1,128)}, s32[1,1,16,512]{3,1,2,0:T(1,128)S(1)}, u32[]{:S(2)}) copy-start(s32[1,1,16,512]{3,1,2,0:T(1,128)S(1)} %copy.86) | copy-start | bytes 98308
  1196.1 45.7 %copy-start.16 = (f32[16,512]{1,0:T(8,128)S(1)}, f32[16,512]{1,0:T(8,128)}, u32[]{:S(2)}) copy-start(f32[16,512]{1,0:T(8,128)} %get-tuple-element.54) | copy-start | bytes 98308
  1196.1 45.7 %copy-start.25 = (f32[768]{0:T(1024)S(1)}, f32[768]{0:T(1024)}, u32[]{:S(2)}) copy-start(f32[768]{0:T(1024)} %get-tuple-element.31) | copy-start | bytes 9220
  1256.1 24.6 copy-start.5
  1281.8 138.6 %copy-start.11 = (s32[8192]{0:T(1024)S(1)}, s32[8192]{0:T(1024)}, u32[]{:S(2)}) copy-start(s32[8192]{0:T(1024)} %copy-done.10) | copy-start | bytes 98308
  1390.0 54.9 %copy-start.12 = (s32[8192]{0:T(1024)}, s32[8192]{0:T(1024)S(1)}, u32[]{:S(2)}) copy-start(s32[8192]{0:T(1024)S(1)} %get-tuple-element.35) | copy-start | bytes 98308
  1444.9 48.5 %copy-start.29 = (pred[8192]{0:T(1024)(128)(4,1)S(1)}, pred[8192]{0:T(1024)(128)(4,1)}, u32[]{:S(2)}) copy-start(pred[8192]{0:T(1024)(128)(4,1)} %get-tuple-element.40) | copy-start | bytes 24580
  1703.5 69.1 %copy-start.36 = (bf16[2,768,768]{2,1,0:T(8,128)(2,1)S(1)}, bf16[2,768,768]{2,1,0:T(8,128)(2,1)}, u32[]{:S(2)}) copy-start(bf16[2,768,768]{2,1,0:T(8,128)(2,1)} %param.26) | copy-start | bytes 7077892
  1772.7 24.4 copy-start.22
  1808.8 79.3 %copy-start.20 = (pred[16384]{0:T(1024)(128)(4,1)S(1)}, pred[16384]{0:T(1024)(128)(4,1)}, u32[]{:S(2)}) copy-start(pred[16384]{0:T(1024)(128)(4,1)} %compare_and_fusion) | copy-start | bytes 49156
  2424.2 281.2 %all-to-all-start.3 = ((bf16[2,8192,768]{2,0,1:T(2,128)(2,1)}), bf16[2,8192,768]{2,0,1:T(2,128)(2,1)}, u32[]{:S(2)}, u32[]{:S(2)}) async-start(bf16[2,8192,768]{2,0,1:T(2,128)(2,1)} %copy.77), calls=%async_computation.3 | async-start | bytes 50331648 | tf_op jit(solution)/shard_map/all_to_all | solution.py:86
  2446.5 24.7 copy-start
  2471.2 65.6 %copy-start.7 = (s32[1,1,16,512]{3,1,2,0:T(1,128)S(1)}, s32[1,1,16,512]{3,1,2,0:T(1,128)}, u32[]{:S(2)}) copy-start(s32[1,1,16,512]{3,1,2,0:T(1,128)} %copy-done.6) | copy-start | bytes 98308
  2728.2 48.5 %copy-start.26 = (pred[8192]{0:T(1024)(128)(4,1)S(1)}, pred[8192]{0:T(1024)(128)(4,1)}, u32[]{:S(2)}) copy-start(pred[8192]{0:T(1024)(128)(4,1)} %get-tuple-element.34) | copy-start | bytes 24580
  (15 other events, 187.0 us)
where the time goes:
time: 2810 us; the launch traced here: 2790 us
  local copies, waits for them, and re-layouts  900 us (32%)
  matrix products  871 us (31%)
  blocking collectives  558 us (20%)
  other arithmetic  279 us (10%)
  waiting for transfers between devices  169 us (6%)
    all_to_all x2, blocking collectives, per_device(): received = lax.all_to_all(packed, 'ep', 0, 1, tiled=True)  558 us
    sub x2, matrix products, attention(): attn_probs = jax.nn.softmax(scores, axis=-1).astype(jnp.bfloat16)  196 us
    dot_general x2, matrix products, expert_ffn(): jnp.einsum('ecf,efd->ecd', inner_act, down_w, preferred_element_type=jnp....  177 us
    dot_general x2, matrix products, expert_ffn(): jnp.einsum('ecd,edf->ecf', rows_in, up_w, preferred_element_type=jnp.floa...  175 us
    all_to_all x2, waiting for transfers between devices, per_device(): returned = lax.all_to_all(expert_rows, 'ep', 1, 0, tiled=True)  169 us
    gather x2, local copies, waits for them, and re-layouts, dispatch(): jnp.take(normed32.astype(jnp.bfloat16), slot_token, axis=0, mode='fill',...  159 us
    dot_general x2, matrix products, attention(): jnp.einsum('shqk,skhd->sqhd', attn_probs, value_rows, preferred_element_t...  138 us
    gather x2, local copies, waits for them, and re-layouts, dispatch(): jnp.take_along_axis(jax.nn.softmax(logits, axis=-1), expert_ids[:, None],...  131 us
  transfers between devices with their start and end apart: 2, of which 1 were waited for; matrix products, arithmetic and copies ran while one was open for 14% of the time, Pallas kernels for 0%

commit v1 on v0

v1 whole, which is shorter than its diff:
```python
import functools

import jax
import jax.numpy as jnp
import numpy as np
from jax import lax
from jax.experimental import pallas as pl
from jax.experimental.pallas import tpu as pltpu
from jax.sharding import PartitionSpec as P

NORM_EPS = 1e-6
NEG_BIG = -1e9
CAP_FACTOR = 2
TILE = 16
BF16 = jnp.bfloat16
F32 = jnp.float32


def neg_pieces():
    pieces, rest = [], np.float32(NEG_BIG)
    for _ in range(3):
        piece = np.float32(np.asarray(rest, jnp.bfloat16))
        pieces.append(float(piece))
        rest = np.float32(rest - piece)
    return pieces


def dot(a, b):
    return jnp.dot(a, b, preferred_element_type=F32)


def dot_t(a, b):
    return lax.dot_general(a, b, (((1,), (1,)), ((), ())), preferred_element_type=F32)


def attention_kernel(x_ref, mask_ref, bias_ref, g0_ref, g1_ref, wq_ref, wk_ref, wv_ref, wo_ref, wr_ref, eid_ref,
                     h1_ref, b_ref, gate_ref, q_s, k_s, v_s, c_s):
    seq, dim = x_ref.shape
    heads = bias_ref.shape[0]
    head = dim // heads
    lanes = 2 * head
    hid = x_ref[...].astype(F32)
    inv = lax.rsqrt(jnp.mean(hid * hid, axis=-1, keepdims=True) + NORM_EPS)
    normed = (hid * inv * g0_ref[...]).astype(BF16)
    q_s[...] = dot(normed, wq_ref[...]).astype(BF16)
    k_s[...] = dot(normed, wk_ref[...]).astype(BF16)
    v_s[...] = dot(normed, wv_ref[...]).astype(BF16)
    lane = lax.broadcasted_iota(jnp.int32, (seq, lanes), 1)
    hi, mid, lo = neg_pieces()
    piece = jnp.where(lane == 0, hi, jnp.where(lane == 1, mid, jnp.where(lane == 2, lo, 0.0)))
    key_mask = jnp.where(mask_ref[...] > 0, 0.0, piece).astype(BF16)
    ones = jnp.ones((seq, lanes), BF16)
    zero = jnp.zeros((seq, lanes), BF16)
    low = lane < head
    for pair in range(heads // 2):
        cols = slice(pair * lanes, (pair + 1) * lanes)
        keys = jnp.concatenate([k_s[:, cols], key_mask], axis=1)
        vals = v_s[:, cols]
        outs = []
        for half in range(2):
            keep = low if half == 0 else jnp.logical_not(low)
            query = jnp.concatenate([jnp.where(keep, q_s[:, cols], zero), ones], axis=1)
            scores = dot_t(query, keys) + bias_ref[2 * pair + half]
            top = jnp.max(scores, axis=-1, keepdims=True)
            probs = jnp.exp(scores - top)
            total = jnp.sum(probs, axis=-1, keepdims=True)
            outs.append(dot(probs.astype(BF16), vals) * (1.0 / total))
        c_s[:, cols] = jnp.where(low, outs[0], outs[1]).astype(BF16)
    h1 = (hid + dot(c_s[...], wo_ref[...])).astype(BF16)
    h1_ref[...] = h1
    hid1 = h1.astype(F32)
    inv1 = lax.rsqrt(jnp.mean(hid1 * hid1, axis=-1, keepdims=True) + NORM_EPS)
    rows = hid1 * inv1 * g1_ref[...]
    rows1 = rows.astype(BF16)
    b_ref[...] = rows1
    rest = rows - rows1.astype(F32)
    rows2 = rest.astype(BF16)
    rows3 = (rest - rows2.astype(F32)).astype(BF16)
    acc = dot(rows1, wr_ref[0]) + (dot(rows2, wr_ref[1]) + dot(rows3, wr_ref[2]))
    nexp = wr_ref.shape[2] // 8
    logits = acc[:, :nexp] + (acc[:, nexp:2 * nexp] + acc[:, 2 * nexp:3 * nexp])
    expo = jnp.exp(logits - jnp.max(logits, axis=-1, keepdims=True))
    ids = lax.broadcasted_iota(jnp.int32, expo.shape, 1)
    picked = jnp.sum(jnp.where(ids == eid_ref[...], expo, 0.0), axis=-1, keepdims=True)
    gate_ref[...] = picked / jnp.sum(expo, axis=-1, keepdims=True)


def attention(hidden, mask_col, rel_bias, g0, g1, wq, wk, wv, wo, wr, eid_col, seq):
    toks, dim = hidden.shape
    heads = rel_bias.shape[0]
    tok_spec = pl.BlockSpec((seq, dim), lambda s: (s, 0))
    col_spec = pl.BlockSpec((seq, 1), lambda s: (s, 0))

    def whole(arr):
        return pl.BlockSpec(arr.shape, lambda s: (0,) * arr.ndim, pipeline_mode=pl.Buffered(1))

    nseq = toks // seq
    return pl.pallas_call(
        attention_kernel,
        grid=(nseq,),
        in_specs=[tok_spec, col_spec, whole(rel_bias), whole(g0), whole(g1), whole(wq), whole(wk), whole(wv), whole(wo),
                  whole(wr), col_spec],
        out_specs=[tok_spec, tok_spec, col_spec],
        out_shape=[jax.ShapeDtypeStruct((toks, dim), BF16), jax.ShapeDtypeStruct((toks, dim), BF16),
                   jax.ShapeDtypeStruct((toks, 1), F32)],
        scratch_shapes=[pltpu.VMEM((seq, dim), BF16)] * 4,
        compiler_params=pltpu.CompilerParams(dimension_semantics=("arbitrary",), vmem_limit_bytes=60 * 2**20),
        cost_estimate=pl.CostEstimate(flops=toks * dim * dim * 8 + toks * seq * dim * 4, bytes_accessed=toks * dim * 6,
                                      transcendentals=toks * seq * heads),
        name="attention",
    )(hidden, mask_col, rel_bias, g0, g1, wq, wk, wv, wo, wr, eid_col)


def pack_kernel(reg_ref, dst_ref, cnt_ref, b_ref, pos_ref, out_ref, acc_s, srt_s, sem, *, nexp, cap):
    step = pl.program_id(0)
    seq, dim = b_ref.shape
    rows = srt_s.shape[0]
    chunk = 256

    @pl.when(step == 0)
    def _():
        def clear(i, carry):
            acc_s[pl.ds(pl.multiple_of(i * chunk, chunk), chunk), :] = jnp.zeros((chunk, dim), BF16)
            return carry
        lax.fori_loop(0, acc_s.shape[0] // chunk, clear, 0)

    pos = pos_ref[0]
    last = step * nexp + nexp - 1
    used = (reg_ref[last] + cnt_ref[last]) * TILE
    for c in range(rows // chunk):
        @pl.when(used > c * chunk)
        def _():
            ids = lax.broadcasted_iota(jnp.int32, (chunk, seq), 0) + c * chunk
            pick = jnp.where(ids == pos, 1.0, 0.0).astype(BF16)
            srt_s[c * chunk:(c + 1) * chunk, :] = dot(pick, b_ref[...]).astype(BF16)

    for e in range(nexp):
        base = step * nexp + e
        src0, dst0 = reg_ref[base] * TILE, dst_ref[base] * TILE + e * cap

        def move(i, carry):
            src = pl.ds(pl.multiple_of(src0 + i * TILE, TILE), TILE)
            dst = pl.ds(pl.multiple_of(dst0 + i * TILE, TILE), TILE)
            acc_s[dst, :] = acc_s[dst, :] + srt_s[src, :]
            return carry
        lax.fori_loop(0, cnt_ref[base], move, 0)

    @pl.when(step == pl.num_programs(0) - 1)
    def _():
        copy = pltpu.make_async_copy(acc_s, out_ref, sem)
        copy.start()
        copy.wait()


def pack(reg, dst, cnt, b, pos_row, nexp, cap):
    toks, dim = b.shape
    nseq, _, seq = pos_row.shape
    rows = seq + 2 * nexp * TILE
    return pl.pallas_call(
        functools.partial(pack_kernel, nexp=nexp, cap=cap),
        grid_spec=pltpu.PrefetchScalarGridSpec(
            num_scalar_prefetch=3,
            grid=(nseq,),
            in_specs=[pl.BlockSpec((seq, dim), lambda s, *_: (s, 0)), pl.BlockSpec((1, 1, seq), lambda s, *_: (s, 0, 0))],
            out_specs=pl.BlockSpec(memory_space=pl.ANY),
            scratch_shapes=[pltpu.VMEM((nexp * cap, dim), BF16), pltpu.VMEM((rows, dim), BF16), pltpu.SemaphoreType.DMA(())],
        ),
        out_shape=jax.ShapeDtypeStruct((nexp * cap, dim), BF16),
        compiler_params=pltpu.CompilerParams(dimension_semantics=("arbitrary",), vmem_limit_bytes=60 * 2**20),
        cost_estimate=pl.CostEstimate(flops=2 * nseq * rows * seq * dim, bytes_accessed=nexp * cap * dim * 2, transcendentals=0),
        name="pack",
    )(reg, dst, cnt, b, pos_row)


def combine_kernel(reg_ref, dst_ref, cnt_ref, ret_ref, h1_ref, gate_ref, pos_ref, out_ref, srt_s, *, nexp, cap):
    step = pl.program_id(0)
    seq, dim = h1_ref.shape
    rows = srt_s.shape[0]

    @pl.when(step == 0)
    def _():
        srt_s[...] = jnp.zeros_like(srt_s)

    for e in range(nexp):
        base = step * nexp + e
        src0, dst0 = reg_ref[base] * TILE, dst_ref[base] * TILE + e * cap

        def move(i, carry):
            src = pl.ds(pl.multiple_of(src0 + i * TILE, TILE), TILE)
            dst = pl.ds(pl.multiple_of(dst0 + i * TILE, TILE), TILE)
            srt_s[src, :] = ret_ref[dst, :]
            return carry
        lax.fori_loop(0, cnt_ref[base], move, 0)

    ids = lax.broadcasted_iota(jnp.int32, (seq, rows), 1)
    pick = jnp.where(ids == pos_ref[...], 1.0, 0.0).astype(BF16)
    back = dot(pick, srt_s[...])
    out_ref[...] = (h1_ref[...].astype(F32) + gate_ref[...] * back).astype(BF16)


def combine(reg, dst, cnt, returned, h1, gate, pos_col, nexp, cap, seq):
    toks, dim = h1.shape
    rows = seq + 2 * nexp * TILE
    tok_spec = pl.BlockSpec((seq, dim), lambda s, *_: (s, 0))
    col_spec = pl.BlockSpec((seq, 1), lambda s, *_: (s, 0))
    return pl.pallas_call(
        functools.partial(combine_kernel, nexp=nexp, cap=cap),
        grid_spec=pltpu.PrefetchScalarGridSpec(
            num_scalar_prefetch=3,
            grid=(toks // seq,),
            in_specs=[pl.BlockSpec(returned.shape, lambda s, *_: (0, 0), pipeline_mode=pl.Buffered(1)), tok_spec, col_spec, col_spec],
            out_specs=tok_spec,
            scratch_shapes=[pltpu.VMEM((rows, dim), BF16)],
        ),
        out_shape=jax.ShapeDtypeStruct((toks, dim), BF16),
        compiler_params=pltpu.CompilerParams(dimension_semantics=("arbitrary",), vmem_limit_bytes=60 * 2**20),
        cost_estimate=pl.CostEstimate(flops=2 * toks * rows * dim, bytes_accessed=nexp * cap * dim * 2, transcendentals=0),
        name="combine",
    )(reg, dst, cnt, returned, h1, gate, pos_col)


def peer_of(k, count):
    me = lax.axis_index('ep')
    chip, core = me // 2, me % 2
    return ((chip + k // 2) % (count // 2)) * 2 + (core + k % 2) % 2


def source_of(k, count):
    me = lax.axis_index('ep')
    chip, core = me // 2, me % 2
    return ((chip + count // 2 - k // 2) % (count // 2)) * 2 + (core + k % 2) % 2


def exchange_kernel(packed_ref, up_ref, down_ref, ret_ref, recv_s, up_s, down_s, acc_s, w_sem, send_sem, recv_sem, back_sem, home_sem,
                    *, layer, count, local, block):
    cap, dim = packed_ref.shape[1], packed_ref.shape[2]
    inner = up_s.shape[2]
    halves = cap // block
    pieces = local * halves
    step = min(inner, 768)
    me = lax.axis_index('ep')

    def part(p):
        return p // halves, pl.ds(pl.multiple_of((p % halves) * block, block), block)

    def outgoing(k, p):
        peer = peer_of(k, count)
        j, rows = part(p)
        return pltpu.make_async_remote_copy(
            src_ref=packed_ref.at[peer * local + j, rows], dst_ref=recv_s.at[k, j, rows], send_sem=send_sem.at[k, p],
            recv_sem=recv_sem.at[k, p], device_id={'ep': peer}, device_id_type=pl.DeviceIdType.MESH)

    def homing(k, p):
        j, rows = part(p)
        return pltpu.make_async_remote_copy(
            src_ref=recv_s.at[k, j, rows], dst_ref=ret_ref.at[me * local + j, rows], send_sem=back_sem.at[k, p],
            recv_sem=home_sem.at[k, p], device_id={'ep': source_of(k, count)}, device_id_type=pl.DeviceIdType.MESH)

    def own_in(p):
        j, rows = part(p)
        return pltpu.make_async_copy(packed_ref.at[me * local + j, rows], recv_s.at[0, j, rows], recv_sem.at[0, p])

    def own_out(p):
        j, rows = part(p)
        return pltpu.make_async_copy(recv_s.at[0, j, rows], ret_ref.at[me * local + j, rows], back_sem.at[0, p])

    def weights(j):
        return (pltpu.make_async_copy(up_ref.at[layer, j], up_s.at[j], w_sem.at[0, j]),
                pltpu.make_async_copy(down_ref.at[layer, j], down_s.at[j], w_sem.at[1, j]))

    barrier = pltpu.get_barrier_semaphore()
    for k in range(1, count):
        pl.semaphore_signal(barrier, inc=1, device_id={'ep': peer_of(k, count)}, device_id_type=pl.DeviceIdType.MESH)
    pl.semaphore_wait(barrier, count - 1)

    def start_out(i, carry):
        outgoing(1 + i % (count - 1), i // (count - 1)).start()
        return carry
    lax.fori_loop(0, pieces * (count - 1), start_out, 0)
    for p in range(pieces):
        own_in(p).start()
    for j in range(local):
        for copy in weights(j):
            copy.start()
    for j in range(local):
        for copy in weights(j):
            copy.wait()

    def order(t):
        u = jnp.maximum(t - pieces, 0)
        own = t < pieces
        return jnp.where(own, 0, 1 + u % (count - 1)), jnp.where(own, t, u // (count - 1))

    def send_back(t):
        @pl.when(t < pieces)
        def _():
            own_out(t).start()

        @pl.when(t >= pieces)
        def _():
            u = t - pieces
            homing(1 + u % (count - 1), u // (count - 1)).start()

    def work(t, carry):
        @pl.when(t < pieces)
        def _():
            own_in(t).wait()

        @pl.when(t >= pieces)
        def _():
            u = t - pieces
            outgoing(1 + u % (count - 1), u // (count - 1)).wait_recv()

        k, p = order(t)
        j, rows = part(p)
        x = recv_s[k, j, rows, :]
        for f in range(0, inner, step):
            act = jnp.maximum(dot(x, up_s[j, :, f:f + step]), 0.0).astype(BF16)
            piece = dot(act, down_s[j, f:f + step, :])
            acc_s[...] = piece if f == 0 else acc_s[...] + piece
        recv_s[k, j, rows, :] = acc_s[...].astype(BF16)

        @pl.when(t > 0)
        def _():
            send_back(t - 1)
        return carry
    total = pieces * count
    lax.fori_loop(0, total, work, 0)
    send_back(total - 1)

    def drain(i, carry):
        k, p = 1 + i % (count - 1), i // (count - 1)
        outgoing(k, p).wait_send()
        back = homing(k, p)
        back.wait_send()
        back.wait_recv()
        return carry
    lax.fori_loop(0, pieces * (count - 1), drain, 0)
    for p in range(pieces):
        own_out(p).wait()


def exchange_ffn(packed, w_in, w_out, layer, count, block=512):
    nexp, cap, dim = packed.shape
    local, inner = w_in.shape[1], w_in.shape[3]
    pieces = local * (cap // block)
    dma = pltpu.SemaphoreType.DMA
    return pl.pallas_call(
        functools.partial(exchange_kernel, layer=layer, count=count, local=local, block=block),
        in_specs=[pl.BlockSpec(memory_space=pl.ANY)] * 3,
        out_specs=pl.BlockSpec(memory_space=pl.ANY),
        out_shape=jax.ShapeDtypeStruct(packed.shape, BF16),
        scratch_shapes=[pltpu.VMEM((count, local, cap, dim), BF16), pltpu.VMEM((local, dim, inner), BF16),
                        pltpu.VMEM((local, inner, dim), BF16), pltpu.VMEM((block, dim), F32), dma((2, local)),
                        dma((count, pieces)), dma((count, pieces)), dma((count, pieces)), dma((count, pieces))],
        compiler_params=pltpu.CompilerParams(collective_id=layer, has_side_effects=True, vmem_limit_bytes=60 * 2**20),
        cost_estimate=pl.CostEstimate(flops=4 * nexp * cap * dim * inner, bytes_accessed=nexp * cap * dim * 4, transcendentals=0),
        name="exchange_ffn",
    )(packed, w_in, w_out)


def routing(expert_idx, nexp, cap):
    layers, nseq, seq = expert_idx.shape
    hot = expert_idx[..., None] == jnp.arange(nexp, dtype=jnp.int32)
    tri = (jnp.arange(seq)[:, None] > jnp.arange(seq)[None, :]).astype(BF16)
    before = jnp.einsum('ut,lste->lsue', tri, hot.astype(BF16), preferred_element_type=F32).astype(jnp.int32)
    count = jnp.sum(hot.astype(jnp.int32), axis=2)
    prior = jnp.arange(nseq)[:, None] > jnp.arange(nseq)[None, :]
    start = jnp.sum(jnp.where(prior[None, :, :, None], count[:, None], 0), axis=2)
    kept = jnp.clip(cap - start, 0, count)
    off = start % TILE
    tiles = jnp.where(kept > 0, (off + kept + TILE - 1) // TILE, 0)
    lower = jnp.arange(nexp)[:, None] > jnp.arange(nexp)[None, :]
    reg = jnp.sum(jnp.where(lower[None, None], tiles[:, :, None, :], 0), axis=3)
    dst = jnp.minimum(start, cap - 1) // TILE
    place = jnp.where(before < kept[:, :, None, :], (reg * TILE + off)[:, :, None, :] + before, 1 << 20)
    pos = jnp.sum(jnp.where(hot, place, 0), axis=3)
    return reg, dst, tiles, pos


def split_router(w_router):
    layers, dim, nexp = w_router.shape
    w1 = lax.reduce_precision(w_router, 8, 7)
    w2 = lax.reduce_precision(w_router - w1, 8, 7)
    w3 = lax.reduce_precision(w_router - w1 - w2, 8, 7)
    zero = jnp.zeros_like(w1)
    rows = [[w1, w2, w3], [w1, w2, zero], [w1, zero, zero]]
    out = jnp.stack([jnp.concatenate(r + [zero] * 5, axis=2) for r in rows], axis=1)
    return out.astype(BF16)


def solution(mesh):
    token_spec = P(('dp', 'ep'))

    def per_device(x_in, pad_mask, rel_bias, expert_idx, norm_scale, w_query, w_key, w_value, w_attn_out, w_router, w_in, w_out):
        num_seqs, seq_len, model_dim = x_in.shape
        toks = num_seqs * seq_len
        nexp = w_router.shape[2]
        layers = w_router.shape[0]
        cap = (CAP_FACTOR * toks + nexp - 1) // nexp
        local = w_in.shape[1]
        count = nexp // local
        reg, dst, tiles, pos = routing(expert_idx, nexp, cap)
        wr = split_router(w_router)
        mask_col = pad_mask.reshape(toks, 1)
        hidden = x_in.reshape(toks, model_dim)
        for layer in range(layers):
            tables = [t[layer].reshape(num_seqs * nexp) for t in (reg, dst, tiles)]
            h1, b, gate = attention(hidden, mask_col, rel_bias, norm_scale[layer, 0][None], norm_scale[layer, 1][None],
                                    w_query[layer], w_key[layer], w_value[layer], w_attn_out[layer], wr[layer],
                                    expert_idx[layer].reshape(toks, 1), seq_len)
            packed = pack(*tables, b, pos[layer].reshape(num_seqs, 1, seq_len), nexp, cap)
            returned = exchange_ffn(packed.reshape(nexp, cap, model_dim), w_in, w_out, layer, count)
            hidden = combine(*tables, returned.reshape(nexp * cap, model_dim), h1, gate, pos[layer].reshape(toks, 1), nexp, cap, seq_len)
        return hidden.reshape(num_seqs, seq_len, model_dim)

    return jax.shard_map(per_device, mesh=mesh, in_specs=(token_spec, token_spec, P(), P(None, ('dp', 'ep')), P(), P(), P(), P(), P(), P(), P(None, 'ep'), P(None, 'ep')), out_specs=token_spec, check_vma=False)
```

time: 2810 us -> 1600 us (0.57)
  Pallas kernels: 0 us -> 1560 us
  local copies, waits for them, and re-layouts: 900 us -> 28 us
  matrix products: 871 us -> 0.74 us
  blocking collectives: 558 us -> 0 us
  other arithmetic: 279 us -> 3.26 us
  waiting for transfers between devices: 169 us -> 0 us
    pallas_call x0 -> x8, Pallas kernels: none -> 1560 us  [the longest x2 1090 us: exchange_ffn(): pl.pallas_call(functools.partial(exchange_kernel, layer=layer, count=coun...]
    dot_general x16 -> x1, matrix products: 675 us -> 0.74 us  [routing(): jnp.einsum('ut,lste->lsue', tri, hot.astype(BF16), preferred_element_type...]
    all_to_all x2 -> x0, blocking collectives: 558 us -> none  [per_device(): received = lax.all_to_all(packed, 'ep', 0, 1, tiled=True)]
    gather x10 -> x0, local copies, waits for them, and re-layouts: 479 us -> none  [the longest x2 159 us: dispatch(): jnp.take(normed32.astype(jnp.bfloat16), slot_token, axis=0, mode='fill',...]
    sub x2 -> x0, matrix products: 196 us -> none  [attention(): attn_probs = jax.nn.softmax(scores, axis=-1).astype(jnp.bfloat16)]
    convert_element_type x8 -> x0, local copies, waits for them, and re-layouts: 192 us -> none  [the longest x6 100 us: project(): out_rows.astype(jnp.bfloat16)]
    all_to_all x2 -> x0, waiting for transfers between devices: 169 us -> none  [per_device(): returned = lax.all_to_all(expert_rows, 'ep', 1, 0, tiled=True)]
    scatter x4 -> x0, local copies, waits for them, and re-layouts: 122 us -> none  [the longest x2 61 us: token_slots(): return jnp.zeros((tok_count,), jnp.int32).at[sort_order].set(rank_sorted)]
  transfers between devices with their start and end apart: 2 -> 0, of which waited for: 1 -> 0; matrix products, arithmetic and copies ran while one was open for 14% -> 0% of each run, Pallas kernels for 0% -> 0%
where the time goes in v1:
time: 1600 us; the launch traced here: 1590 us
  Pallas kernels  1560 us (98%)
  local copies, waits for them, and re-layouts  28 us (2%)
    pallas_call x2, Pallas kernels, exchange_ffn(): pl.pallas_call(functools.partial(exchange_kernel, layer=layer, count=coun...  1090 us
    pallas_call x2, Pallas kernels, attention(): pl.pallas_call(attention_kernel, grid=(nseq,), in_specs=[tok_spec, col_sp...  323 us
    pallas_call x2, Pallas kernels, pack(): pl.pallas_call(functools.partial(pack_kernel, nexp=nexp, cap=cap), grid_s...  74.5 us
    pallas_call x2, Pallas kernels, combine(): pl.pallas_call(functools.partial(combine_kernel, nexp=nexp, cap=cap), gri...  68.9 us

profile of v1, /device:TPU:113, one launch (start us, length us, event | category | flops | bytes accessed | tf_op | source)
XLA Modules:
  0.0 1592.4 jit_solution(17398367284114009895)
XLA Ops:
  0.0 1.6 convert_reduce_fusion
  3.7 0.7 reshape_squeeze.38.cnt_ref
  5.0 0.6 reshape_squeeze.40.dst_ref
  5.6 0.7 reshape_squeeze.41.cnt_ref
  6.3 0.8 copy.67
  7.1 2.6 copy.68
  9.7 0.6 slice_bitcast_fusion.12
  10.3 4.1 slice_bitcast_fusion.2
  14.4 2.3 slice_bitcast_fusion
  18.3 1.1 slice_bitcast_fusion.8
  20.1 2.6 copy.70
  22.7 161.7 %attention.2 = (bf16[8192,768]{1,0:T(8,128)(2,1)}, bf16[8192,768]{1,0:T(8,128)(2,1)}, f32[8192,1]{1,0:T(8,128)}) custom-call(bf16[8192,768]{1,0:T(8,128)(2,1)} %bitcast.81, s32[8192,1]{1,0:T(8,128)} %bitcast.71, f32[12,512,512]{2,1,0:T(8,128)} %bias_ref.3, f32[1,768]{1,0:T(1,128)} %get-tuple-element.52.g0_ref, f32[1,768]{1,0:T(1,128)} %get-tuple-element.51.g1_ref, ...), custom_call_target="tpu_custom_call" | custom-call | flops 51539607552 | bytes 37748736 | tf_op jit(solution)/shard_map/attention/pallas_call | solution.py:98
  184.4 0.7 fusion
  185.2 0.7 fusion.15
  185.9 37.2 %pack.2 = bf16[16384,768]{1,0:T(8,128)(2,1)} custom-call(s32[256]{0:T(256)} %reshape_squeeze.39.reg_ref, s32[256]{0:T(256)} %reshape_squeeze.40.dst_ref, s32[256]{0:T(256)} %reshape_squeeze.41.cnt_ref, bf16[8192,768]{1,0:T(8,128)(2,1)} %get-tuple-element.11.b_ref, s32[16,1,512]{2,1,0:T(1,128)} %get-tuple-element.60.pos_ref), custom_call_target="tpu_custom_call" | custom-call | flops 12884901888 | bytes 25165824 | tf_op jit(solution)/shard_map/pack/pallas_call | solution.py:159
  223.1 546.3 %exchange_ffn.2 = bf16[16,1024,768]{2,1,0:T(8,128)(2,1)} custom-call(bf16[16,1024,768]{2,1,0:T(8,128)(2,1)} %bitcast.82, bf16[2,2,768,3072]{3,2,1,0:T(8,128)(2,1)} %up_ref.3, bf16[2,2,3072,768]{3,2,1,0:T(8,128)(2,1)} %down_ref.3), custom_call_target="tpu_custom_call" | custom-call | flops 154618822656 | bytes 50331648 | tf_op jit(solution)/shard_map/exchange_ffn/pallas_call | solution.py:348
  769.4 2.6 copy.59.pos_ref
  772.1 34.5 %combine.2.x_ref = bf16[8192,768]{1,0:T(8,128)(2,1)} custom-call(s32[256]{0:T(256)} %reshape_squeeze.39.reg_ref, s32[256]{0:T(256)} %reshape_squeeze.40.dst_ref, s32[256]{0:T(256)} %reshape_squeeze.41.cnt_ref, bf16[16384,768]{1,0:T(8,128)(2,1)} %bitcast.70, bf16[8192,768]{1,0:T(8,128)(2,1)} %get-tuple-element.12.h1_ref, ...), custom_call_target="tpu_custom_call" | custom-call | flops 12884901888 | bytes 25165824 | tf_op jit(solution)/shard_map/combine/pallas_call | solution.py:206
  806.6 2.6 copy.72
  809.2 161.7 %attention.3 = (bf16[8192,768]{1,0:T(8,128)(2,1)}, bf16[8192,768]{1,0:T(8,128)(2,1)}, f32[8192,1]{1,0:T(8,128)}) custom-call(bf16[8192,768]{1,0:T(8,128)(2,1)} %combine.2.x_ref, s32[8192,1]{1,0:T(8,128)} %bitcast.72, f32[12,512,512]{2,1,0:T(8,128)} %bias_ref.3, f32[1,768]{1,0:T(1,128)} %get-tuple-element.53.g0_ref, f32[1,768]{1,0:T(1,128)} %get-tuple-element.50.g1_ref, ...), custom_call_target="tpu_custom_call" | custom-call | flops 51539607552 | bytes 37748736 | tf_op jit(solution)/shard_map/attention/pallas_call | solution.py:98
  970.9 37.2 %pack.3 = bf16[16384,768]{1,0:T(8,128)(2,1)} custom-call(s32[256]{0:T(256)} %reshape_squeeze.36.reg_ref, s32[256]{0:T(256)} %reshape_squeeze.37.dst_ref, s32[256]{0:T(256)} %reshape_squeeze.38.cnt_ref, bf16[8192,768]{1,0:T(8,128)(2,1)} %get-tuple-element.14.b_ref, s32[16,1,512]{2,1,0:T(1,128)} %get-tuple-element.38.pos_ref), custom_call_target="tpu_custom_call" | custom-call | flops 12884901888 | bytes 25165824 | tf_op jit(solution)/shard_map/pack/pallas_call | solution.py:159
  1008.2 546.7 %exchange_ffn.3 = bf16[16,1024,768]{2,1,0:T(8,128)(2,1)} custom-call(bf16[16,1024,768]{2,1,0:T(8,128)(2,1)} %bitcast.83, bf16[2,2,768,3072]{3,2,1,0:T(8,128)(2,1)} %up_ref.3, bf16[2,2,3072,768]{3,2,1,0:T(8,128)(2,1)} %down_ref.3), custom_call_target="tpu_custom_call" | custom-call | flops 154618822656 | bytes 50331648 | tf_op jit(solution)/shard_map/exchange_ffn/pallas_call | solution.py:348
  1554.9 2.6 copy.63.pos_ref
  1557.6 34.4 %combine.3 = bf16[8192,768]{1,0:T(8,128)(2,1)} custom-call(s32[256]{0:T(256)} %reshape_squeeze.36.reg_ref, s32[256]{0:T(256)} %reshape_squeeze.37.dst_ref, s32[256]{0:T(256)} %reshape_squeeze.38.cnt_ref, bf16[16384,768]{1,0:T(8,128)(2,1)} %bitcast.69, bf16[8192,768]{1,0:T(8,128)(2,1)} %get-tuple-element.15.h1_ref, f32[8192,1]{1,0:T(8,128)} %get-tuple-element.16.gate_ref, ...), custom_call_target="tpu_custom_call" | custom-call | flops 12884901888 | bytes 25165824 | tf_op jit(solution)/shard_map/combine/pallas_call | solution.py:206
  (42 shorter events, 4.9 us)
Async XLA Ops:
  0.0 9.7 copy-start.8
  0.0 10.3 copy-start
  10.3 4.1 copy-start.1
  10.3 4.1 copy-start.2
  14.4 2.3 copy-start.3
  18.2 1.3 copy-start.4
  223.1 546.3 %copy-start.6 = (s32[1,16,512]{2,0,1:T(1,128)S(1)}, s32[1,16,512]{2,0,1:T(1,128)}, u32[]{:S(2)}) copy-start(s32[1,16,512]{2,0,1:T(1,128)} %get-tuple-element.61) | copy-start | bytes 98308
  772.1 34.5 %copy-start.7 = (s32[1,1,16,512]{3,2,1,0:T(8,128)S(1)}, s32[1,1,16,512]{3,2,1,0:T(8,128)}, u32[]{:S(2)}) copy-start(s32[1,1,16,512]{3,2,1,0:T(8,128)} %get-tuple-element.35) | copy-start | bytes 98308
  1008.2 546.7 %copy-start.5 = (s32[1,16,512]{2,0,1:T(1,128)S(1)}, s32[1,16,512]{2,0,1:T(1,128)}, u32[]{:S(2)}) copy-start(s32[1,16,512]{2,0,1:T(1,128)} %get-tuple-element.37) | copy-start | bytes 98308

commit v2 on v1

--- a/solution.py
+++ b/solution.py
@@ -12,6 +12,8 @@
 NEG_BIG = -1e9
 CAP_FACTOR = 2
 TILE = 16
+PAIRS_PER_STEP = 1
+SHARED = (1, 1)
 BF16 = jnp.bfloat16
 F32 = jnp.float32
 
@@ -42,9 +44,11 @@
     hid = x_ref[...].astype(F32)
     inv = lax.rsqrt(jnp.mean(hid * hid, axis=-1, keepdims=True) + NORM_EPS)
     normed = (hid * inv * g0_ref[...]).astype(BF16)
-    q_s[...] = dot(normed, wq_ref[...]).astype(BF16)
-    k_s[...] = dot(normed, wk_ref[...]).astype(BF16)
-    v_s[...] = dot(normed, wv_ref[...]).astype(BF16)
+    pairs = heads // 2
+    for w_ref, rows_s in ((wq_ref, q_s), (wk_ref, k_s), (wv_ref, v_s)):
+        rows = dot(normed, w_ref[...]).astype(BF16)
+        for pair in range(pairs):
+            rows_s[pair] = rows[:, pair * lanes:(pair + 1) * lanes]
     lane = lax.broadcasted_iota(jnp.int32, (seq, lanes), 1)
     hi, mid, lo = neg_pieces()
     piece = jnp.where(lane == 0, hi, jnp.where(lane == 1, mid, jnp.where(lane == 2, lo, 0.0)))
@@ -52,21 +56,30 @@
     ones = jnp.ones((seq, lanes), BF16)
     zero = jnp.zeros((seq, lanes), BF16)
     low = lane < head
-    for pair in range(heads // 2):
-        cols = slice(pair * lanes, (pair + 1) * lanes)
-        keys = jnp.concatenate([k_s[:, cols], key_mask], axis=1)
-        vals = v_s[:, cols]
+
+    def one_pair(pair):
+        keys = jnp.concatenate([k_s[pair], key_mask], axis=1)
+        vals = v_s[pair]
         outs = []
         for half in range(2):
             keep = low if half == 0 else jnp.logical_not(low)
-            query = jnp.concatenate([jnp.where(keep, q_s[:, cols], zero), ones], axis=1)
+            query = jnp.concatenate([jnp.where(keep, q_s[pair], zero), ones], axis=1)
             scores = dot_t(query, keys) + bias_ref[2 * pair + half]
             top = jnp.max(scores, axis=-1, keepdims=True)
             probs = jnp.exp(scores - top)
             total = jnp.sum(probs, axis=-1, keepdims=True)
             outs.append(dot(probs.astype(BF16), vals) * (1.0 / total))
-        c_s[:, cols] = jnp.where(low, outs[0], outs[1]).astype(BF16)
-    h1 = (hid + dot(c_s[...], wo_ref[...])).astype(BF16)
+        c_s[pair] = jnp.where(low, outs[0], outs[1]).astype(BF16)
+
+    group = PAIRS_PER_STEP
+
+    def some_pairs(i, carry):
+        for n in range(group):
+            one_pair(i * group + n)
+        return carry
+    lax.fori_loop(0, pairs // group, some_pairs, 0)
+    context = jnp.concatenate([c_s[pair] for pair in range(pairs)], axis=1)
+    h1 = (hid + dot(context, wo_ref[...])).astype(BF16)
     h1_ref[...] = h1
     hid1 = h1.astype(F32)
     inv1 = lax.rsqrt(jnp.mean(hid1 * hid1, axis=-1, keepdims=True) + NORM_EPS)
@@ -103,7 +116,7 @@
         out_specs=[tok_spec, tok_spec, col_spec],
         out_shape=[jax.ShapeDtypeStruct((toks, dim), BF16), jax.ShapeDtypeStruct((toks, dim), BF16),
                    jax.ShapeDtypeStruct((toks, 1), F32)],
-        scratch_shapes=[pltpu.VMEM((seq, dim), BF16)] * 4,
+        scratch_shapes=[pltpu.VMEM((heads // 2, seq, 2 * dim // heads), BF16)] * 4,
         compiler_params=pltpu.CompilerParams(dimension_semantics=("arbitrary",), vmem_limit_bytes=60 * 2**20),
         cost_estimate=pl.CostEstimate(flops=toks * dim * dim * 8 + toks * seq * dim * 4, bytes_accessed=toks * dim * 6,
                                       transcendentals=toks * seq * heads),
@@ -231,13 +244,30 @@
     return ((chip + count // 2 - k // 2) % (count // 2)) * 2 + (core + k % 2) % 2
 
 
-def exchange_kernel(packed_ref, up_ref, down_ref, ret_ref, recv_s, up_s, down_s, acc_s, w_sem, send_sem, recv_sem, back_sem, home_sem,
-                    *, layer, count, local, block):
+def expert_rows(x, up, down, acc_s, inner):
+    step = min(inner, 768)
+
+    def part(f, carry):
+        cols = pl.ds(pl.multiple_of(f * step, step), step)
+        act = jnp.maximum(dot(x, up[:, cols]), 0.0).astype(BF16)
+        acc_s[...] = acc_s[...] + dot(act, down[cols, :])
+        return carry
+    acc_s[...] = jnp.zeros_like(acc_s)
+    lax.fori_loop(0, inner // step, part, 0)
+    return acc_s[...].astype(BF16)
+
+
+def exchange_kernel(*refs, layer, count, local, away, block, stay):
+    if stay:
+        (packed_ref, up_ref, down_ref, ups_ref, downs_ref, ret_ref, recv_s, up_s, down_s, acc_s, w_sem, send_sem, recv_sem, back_sem,
+         home_sem, x_h, up_h, down_h, in_sem, out_sem) = refs
+    else:
+        (packed_ref, up_ref, down_ref, ret_ref, recv_s, up_s, down_s, acc_s, w_sem, send_sem, recv_sem, back_sem,
+         home_sem) = refs
     cap, dim = packed_ref.shape[1], packed_ref.shape[2]
     inner = up_s.shape[2]
     halves = cap // block
-    pieces = local * halves
-    step = min(inner, 768)
+    pieces = away * halves
     me = lax.axis_index('ep')
 
     def part(p):
@@ -268,6 +298,15 @@
         return (pltpu.make_async_copy(up_ref.at[layer, j], up_s.at[j], w_sem.at[0, j]),
                 pltpu.make_async_copy(down_ref.at[layer, j], down_s.at[j], w_sem.at[1, j]))
 
+    def home_in(n):
+        slot = n % 2
+        return (pltpu.make_async_copy(packed_ref.at[(n // stay) * local + away + n % stay], x_h.at[slot], in_sem.at[0, slot]),
+                pltpu.make_async_copy(ups_ref.at[n], up_h.at[slot], in_sem.at[1, slot]),
+                pltpu.make_async_copy(downs_ref.at[n], down_h.at[slot], in_sem.at[2, slot]))
+
+    def home_out(n):
+        return pltpu.make_async_copy(x_h.at[n % 2], ret_ref.at[(n // stay) * local + away + n % stay], out_sem.at[n % 2])
+
     barrier = pltpu.get_barrier_semaphore()
     for k in range(1, count):
         pl.semaphore_signal(barrier, inc=1, device_id={'ep': peer_of(k, count)}, device_id_type=pl.DeviceIdType.MESH)
@@ -279,10 +318,13 @@
     lax.fori_loop(0, pieces * (count - 1), start_out, 0)
     for p in range(pieces):
         own_in(p).start()
-    for j in range(local):
+    for j in range(away):
         for copy in weights(j):
             copy.start()
-    for j in range(local):
+    if stay:
+        for copy in home_in(0):
+            copy.start()
+    for j in range(away):
         for copy in weights(j):
             copy.wait()
 
@@ -313,16 +355,36 @@
 
         k, p = order(t)
         j, rows = part(p)
-        x = recv_s[k, j, rows, :]
-        for f in range(0, inner, step):
-            act = jnp.maximum(dot(x, up_s[j, :, f:f + step]), 0.0).astype(BF16)
-            piece = dot(act, down_s[j, f:f + step, :])
-            acc_s[...] = piece if f == 0 else acc_s[...] + piece
-        recv_s[k, j, rows, :] = acc_s[...].astype(BF16)
+        recv_s[k, j, rows, :] = expert_rows(recv_s[k, j, rows, :], up_s.at[j], down_s.at[j], acc_s, inner)
 
         @pl.when(t > 0)
         def _():
             send_back(t - 1)
+
+        if stay:
+            n, i = t // halves, t % halves
+            slot = n % 2
+
+            @pl.when(i == 0)
+            def _():
+                for copy in home_in(n):
+                    copy.wait()
+
+            @pl.when(jnp.logical_and(i == 1, n > 0))
+            def _():
+                home_out(n - 1).wait()
+
+            @pl.when(jnp.logical_and(i == 1, n + 1 < count * stay))
+            def _():
+                for copy in home_in(n + 1):
+                    copy.start()
+
+            mine = pl.ds(pl.multiple_of(i * block, block), block)
+            x_h[slot, mine, :] = expert_rows(x_h[slot, mine, :], up_h.at[slot], down_h.at[slot], acc_s, inner)
+
+            @pl.when(i == halves - 1)
+            def _():
+                home_out(n).start()
         return carry
     total = pieces * count
     lax.fori_loop(0, total, work, 0)
@@ -338,25 +400,71 @@
     lax.fori_loop(0, pieces * (count - 1), drain, 0)
     for p in range(pieces):
         own_out(p).wait()
-
-
-def exchange_ffn(packed, w_in, w_out, layer, count, block=512):
+    if stay:
+        home_out(count * stay - 1).wait()
+
+
+def exchange_ffn(packed, w_in, w_out, layer, count, away, ups=None, downs=None, block=256):
     nexp, cap, dim = packed.shape
     local, inner = w_in.shape[1], w_in.shape[3]
-    pieces = local * (cap // block)
+    pieces = away * (cap // block)
+    stay = 0 if ups is None else local - away
+    assert stay in (0, away) and cap // block > 2
     dma = pltpu.SemaphoreType.DMA
+    scratch = [pltpu.VMEM((count, away, cap, dim), BF16), pltpu.VMEM((away, dim, inner), BF16),
+               pltpu.VMEM((away, inner, dim), BF16), pltpu.VMEM((block, dim), F32), dma((2, away)),
+               dma((count, pieces)), dma((count, pieces)), dma((count, pieces)), dma((count, pieces))]
+    operands = [packed, w_in, w_out]
+    if stay:
+        scratch += [pltpu.VMEM((2, cap, dim), BF16), pltpu.VMEM((2, dim, inner), BF16), pltpu.VMEM((2, inner, dim), BF16),
+                    dma((3, 2)), dma((2,))]
+        operands += [ups, downs]
     return pl.pallas_call(
-        functools.partial(exchange_kernel, layer=layer, count=count, local=local, block=block),
-        in_specs=[pl.BlockSpec(memory_space=pl.ANY)] * 3,
+        functools.partial(exchange_kernel, layer=layer, count=count, local=local, away=away, block=block, stay=stay),
+        in_specs=[pl.BlockSpec(memory_space=pl.ANY)] * len(operands),
         out_specs=pl.BlockSpec(memory_space=pl.ANY),
         out_shape=jax.ShapeDtypeStruct(packed.shape, BF16),
-        scratch_shapes=[pltpu.VMEM((count, local, cap, dim), BF16), pltpu.VMEM((local, dim, inner), BF16),
-                        pltpu.VMEM((local, inner, dim), BF16), pltpu.VMEM((block, dim), F32), dma((2, local)),
-                        dma((count, pieces)), dma((count, pieces)), dma((count, pieces)), dma((count, pieces))],
+        scratch_shapes=scratch,
         compiler_params=pltpu.CompilerParams(collective_id=layer, has_side_effects=True, vmem_limit_bytes=60 * 2**20),
-        cost_estimate=pl.CostEstimate(flops=4 * nexp * cap * dim * inner, bytes_accessed=nexp * cap * dim * 4, transcendentals=0),
+        cost_estimate=pl.CostEstimate(flops=4 * count * (away + stay) * cap * dim * inner, bytes_accessed=nexp * cap * dim * 4,
+                                      transcendentals=0),
         name="exchange_ffn",
-    )(packed, w_in, w_out)
+    )(*operands)
+
+
+def home_kernel(fill_ref, x_ref, up_ref, down_ref, ret_ref, out_ref, acc_s, *, local, away, block):
+    here = pl.program_id(0)
+    e = (here // (local - away)) * local + away + here % (local - away)
+    inner = up_ref.shape[1]
+
+    def work(i, carry):
+        rows = pl.ds(pl.multiple_of(i * block, block), block)
+        out_ref[rows, :] = expert_rows(x_ref[rows, :], up_ref, down_ref, acc_s, inner)
+        return carry
+    lax.fori_loop(0, (fill_ref[e] + block - 1) // block, work, 0)
+
+
+def home_ffn(fill, packed, up, down, ret, local, away, block=256):
+    nexp, cap, dim = packed.shape
+    here, inner = up.shape[0], up.shape[2]
+    stay = local - away
+    row_spec = pl.BlockSpec((None, cap, dim), lambda e, *_: ((e // stay) * local + away + e % stay, 0, 0))
+    return pl.pallas_call(
+        functools.partial(home_kernel, local=local, away=away, block=block),
+        grid_spec=pltpu.PrefetchScalarGridSpec(
+            num_scalar_prefetch=1,
+            grid=(here,),
+            in_specs=[row_spec, pl.BlockSpec((None, dim, inner), lambda e, *_: (e, 0, 0)),
+                      pl.BlockSpec((None, inner, dim), lambda e, *_: (e, 0, 0)), pl.BlockSpec(memory_space=pl.ANY)],
+            out_specs=row_spec,
+            scratch_shapes=[pltpu.VMEM((block, dim), F32)],
+        ),
+        out_shape=jax.ShapeDtypeStruct(packed.shape, BF16),
+        input_output_aliases={4: 0},
+        compiler_params=pltpu.CompilerParams(dimension_semantics=("arbitrary",), vmem_limit_bytes=60 * 2**20),
+        cost_estimate=pl.CostEstimate(flops=2 * here * cap * dim * inner, bytes_accessed=here * cap * dim * 4, transcendentals=0),
+        name="home_ffn",
+    )(fill, packed, up, down, ret)
 
 
 def routing(expert_idx, nexp, cap):
@@ -375,7 +483,7 @@
     dst = jnp.minimum(start, cap - 1) // TILE
     place = jnp.where(before < kept[:, :, None, :], (reg * TILE + off)[:, :, None, :] + before, 1 << 20)
     pos = jnp.sum(jnp.where(hot, place, 0), axis=3)
-    return reg, dst, tiles, pos
+    return reg, dst, tiles, pos, jnp.sum(kept, axis=1)
 
 
 def split_router(w_router):
@@ -400,17 +508,39 @@
         cap = (CAP_FACTOR * toks + nexp - 1) // nexp
         local = w_in.shape[1]
         count = nexp // local
-        reg, dst, tiles, pos = routing(expert_idx, nexp, cap)
+        reg, dst, tiles, pos, fill = routing(expert_idx, nexp, cap)
         wr = split_router(w_router)
         mask_col = pad_mask.reshape(toks, 1)
         hidden = x_in.reshape(toks, model_dim)
+        shared = [min(n, local - 1) for n in SHARED]
+
+        def gather(weight, layer, early, after):
+            if early is not None:
+                weight, _ = lax.optimization_barrier((weight, early))
+            own = weight[layer, local - shared[layer]:]
+            if after is not None:
+                own, _ = lax.optimization_barrier((own, after))
+            return lax.all_gather(own, 'ep', axis=0, tiled=True)
+
+        early = after = None
         for layer in range(layers):
             tables = [t[layer].reshape(num_seqs * nexp) for t in (reg, dst, tiles)]
+            if shared[layer]:
+                ups, downs = (gather(w, layer, early, after) for w in (w_in, w_out))
             h1, b, gate = attention(hidden, mask_col, rel_bias, norm_scale[layer, 0][None], norm_scale[layer, 1][None],
                                     w_query[layer], w_key[layer], w_value[layer], w_attn_out[layer], wr[layer],
                                     expert_idx[layer].reshape(toks, 1), seq_len)
+            early = gate[:8]
             packed = pack(*tables, b, pos[layer].reshape(num_seqs, 1, seq_len), nexp, cap)
-            returned = exchange_ffn(packed.reshape(nexp, cap, model_dim), w_in, w_out, layer, count)
+            packed = packed.reshape(nexp, cap, model_dim)
+            away = local - shared[layer]
+            if shared[layer] and layer == layers - 1:
+                returned = exchange_ffn(packed, w_in, w_out, layer, count, away, ups, downs)
+            else:
+                returned = exchange_ffn(packed, w_in, w_out, layer, count, away)
+                after = returned[0, :TILE, :128]
+                if shared[layer]:
+                    returned = home_ffn(fill[layer], packed, ups, downs, returned, local, away)
             hidden = combine(*tables, returned.reshape(nexp * cap, model_dim), h1, gate, pos[layer].reshape(toks, 1), nexp, cap, seq_len)
         return hidden.reshape(num_seqs, seq_len, model_dim)
 

time: 1600 us -> 1330 us (0.83)
  Pallas kernels: 1560 us -> 1260 us
  local copies, waits for them, and re-layouts: 28 us -> 51 us
    pallas_call x2, Pallas kernels: 1090 us -> 621 us  [exchange_ffn(): pl.pallas_call(functools.partial(exchange_kernel, layer=layer, count=coun...]
    pallas_call x0 -> x1, Pallas kernels: none -> 86.6 us  [home_ffn(): pl.pallas_call(functools.partial(home_kernel, local=local, away=away, blo...]
    pallas_call x2, Pallas kernels: 323 us -> 409 us  [attention(): pl.pallas_call(attention_kernel, grid=(nseq,), in_specs=[tok_spec, col_sp...]
  transfers between devices with their start and end apart: 0 -> 4, of which waited for: 0 -> 0; matrix products, arithmetic and copies ran while one was open for 0% -> 4% of each run, Pallas kernels for 0% -> 71%
where the time goes in v2:
time: 1330 us
  Pallas kernels  1260 us (95%)
  local copies, waits for them, and re-layouts  51 us (4%)
  between operations  13.4 us (1%)
    pallas_call x2, Pallas kernels, exchange_ffn(): pl.pallas_call(functools.partial(exchange_kernel, layer=layer, count=coun...  621 us
    pallas_call x2, Pallas kernels, attention(): pl.pallas_call(attention_kernel, grid=(nseq,), in_specs=[tok_spec, col_sp...  409 us
    pallas_call x1, Pallas kernels, home_ffn(): pl.pallas_call(functools.partial(home_kernel, local=local, away=away, blo...  86.6 us
    pallas_call x2, Pallas kernels, pack(): pl.pallas_call(functools.partial(pack_kernel, nexp=nexp, cap=cap), grid_s...  75.2 us
    pallas_call x2, Pallas kernels, combine(): pl.pallas_call(functools.partial(combine_kernel, nexp=nexp, cap=cap), gri...  68.8 us
  transfers between devices with their start and end apart: 4, of which 0 were waited for; matrix products, arithmetic and copies ran while one was open for 4% of the time, Pallas kernels for 71%

profile of v2, /device:TPU:113, one launch (start us, length us, event | category | flops | bytes accessed | tf_op | source)
XLA Modules:
  0.0 1328.5 jit_solution(3005217057471575862)
XLA Ops:
  6.6 4.8 slice.111
  11.5 4.8 slice.112
  16.5 0.8 copy-done.4
  23.4 2.9 copy.73
  27.3 2.8 copy.75
  31.7 1.1 slice_bitcast_fusion.10
  32.8 2.5 slice_bitcast_fusion.4
  36.0 0.9 copy-done.3
  36.9 2.3 slice_bitcast_fusion.2
  39.2 204.4 %attention.2 = (bf16[8192,768]{1,0:T(8,128)(2,1)}, bf16[8192,768]{1,0:T(8,128)(2,1)}, f32[8192,1]{1,0:T(8,128)}) custom-call(bf16[8192,768]{1,0:T(8,128)(2,1)} %bitcast.95, s32[8192,1]{1,0:T(8,128)} %bitcast.85, f32[12,512,512]{2,1,0:T(8,128)} %bias_ref.3, f32[1,768]{1,0:T(1,128)} %get-tuple-element.61.g0_ref, f32[1,768]{1,0:T(1,128)} %get-tuple-element.60.g1_ref, ...), custom_call_target="tpu_custom_call" | custom-call | flops 51539607552 | bytes 37748736 | tf_op jit(solution)/shard_map/attention/pallas_call | solution.py:111
  243.6 0.7 fusion
  245.1 37.6 %pack.2 = bf16[16384,768]{1,0:T(8,128)(2,1)} custom-call(s32[256]{0:T(256)} %reshape_squeeze.39.reg_ref, s32[256]{0:T(256)} %reshape_squeeze.40.dst_ref, s32[256]{0:T(256)} %reshape_squeeze.41.cnt_ref, bf16[8192,768]{1,0:T(8,128)(2,1)} %get-tuple-element.15.b_ref, s32[16,1,512]{2,1,0:T(1,128)} %get-tuple-element.67.pos_ref), custom_call_target="tpu_custom_call" | custom-call | flops 12884901888 | bytes 25165824 | tf_op jit(solution)/shard_map/pack/pallas_call | solution.py:172
  282.7 344.5 %exchange_ffn.2.ret_ref = bf16[16,1024,768]{2,1,0:T(8,128)(2,1)} custom-call(bf16[16,1024,768]{2,1,0:T(8,128)(2,1)} %bitcast.83, bf16[2,2,768,3072]{3,2,1,0:T(8,128)(2,1)} %refs_1_.3, bf16[2,2,3072,768]{3,2,1,0:T(8,128)(2,1)} %refs_2_.3), custom_call_target="tpu_custom_call" | custom-call | flops 77309411328 | bytes 50331648 | tf_op jit(solution)/shard_map/exchange_ffn/pallas_call | solution.py:422
  627.2 4.9 slice_bitcast_fusion.1
  632.3 4.8 slice_bitcast_fusion
  639.7 2.6 copy.64.pos_ref
  642.3 2.7 copy.77
  645.0 2.8 copy.68.pos_ref
  648.4 86.6 %home_ffn.1 = bf16[16,1024,768]{2,1,0:T(8,128)(2,1)} custom-call(s32[16]{0:T(128)} %slice_bitcast_fusion.19.fill_ref, bf16[16,1024,768]{2,1,0:T(8,128)(2,1)} %bitcast.84, bf16[8,768,3072]{2,1,0:T(8,128)(2,1)} %bitcast.80, bf16[8,3072,768]{2,1,0:T(8,128)(2,1)} %bitcast.81, bf16[16,1024,768]{2,1,0:T(8,128)(2,1)} %exchange_ffn.2.ret_ref), custom_call_target="tpu_custom_call", output_to_operand_aliasing={{}: (4, {})} | custom-call | flops 38654705664 | bytes 25165824 | tf_op jit(solution)/shard_map/home_ffn/pallas_call | solution.py:452
  734.9 34.4 %combine.2.x_ref = bf16[8192,768]{1,0:T(8,128)(2,1)} custom-call(s32[256]{0:T(256)} %reshape_squeeze.39.reg_ref, s32[256]{0:T(256)} %reshape_squeeze.40.dst_ref, s32[256]{0:T(256)} %reshape_squeeze.41.cnt_ref, bf16[16384,768]{1,0:T(8,128)(2,1)} %bitcast.79, bf16[8192,768]{1,0:T(8,128)(2,1)} %get-tuple-element.16.h1_ref, ...), custom_call_target="tpu_custom_call" | custom-call | flops 12884901888 | bytes 25165824 | tf_op jit(solution)/shard_map/combine/pallas_call | solution.py:219
  769.3 204.4 %attention.3 = (bf16[8192,768]{1,0:T(8,128)(2,1)}, bf16[8192,768]{1,0:T(8,128)(2,1)}, f32[8192,1]{1,0:T(8,128)}) custom-call(bf16[8192,768]{1,0:T(8,128)(2,1)} %combine.2.x_ref, s32[8192,1]{1,0:T(8,128)} %bitcast.86, f32[12,512,512]{2,1,0:T(8,128)} %bias_ref.3, f32[1,768]{1,0:T(1,128)} %get-tuple-element.62.g0_ref, f32[1,768]{1,0:T(1,128)} %get-tuple-element.59.g1_ref, ...), custom_call_target="tpu_custom_call" | custom-call | flops 51539607552 | bytes 37748736 | tf_op jit(solution)/shard_map/attention/pallas_call | solution.py:111
  973.8 37.6 %pack.3 = bf16[16384,768]{1,0:T(8,128)(2,1)} custom-call(s32[256]{0:T(256)} %reshape_squeeze.36.reg_ref, s32[256]{0:T(256)} %reshape_squeeze.37.dst_ref, s32[256]{0:T(256)} %reshape_squeeze.38.cnt_ref, bf16[8192,768]{1,0:T(8,128)(2,1)} %get-tuple-element.18.b_ref, s32[16,1,512]{2,1,0:T(1,128)} %get-tuple-element.48.pos_ref), custom_call_target="tpu_custom_call" | custom-call | flops 12884901888 | bytes 25165824 | tf_op jit(solution)/shard_map/pack/pallas_call | solution.py:172
  1011.4 276.2 %exchange_ffn.3 = bf16[16,1024,768]{2,1,0:T(8,128)(2,1)} custom-call(bf16[16,1024,768]{2,1,0:T(8,128)(2,1)} %bitcast.96, bf16[2,2,768,3072]{3,2,1,0:T(8,128)(2,1)} %refs_1_.3, bf16[2,2,3072,768]{3,2,1,0:T(8,128)(2,1)} %refs_2_.3, bf16[8,768,3072]{2,1,0:T(8,128)(2,1)} %all-gather.7.cloned.1.call-done.refs_3_, ...), custom_call_target="tpu_custom_call" | custom-call | flops 154618822656 | bytes 50331648 | tf_op jit(solution)/shard_map/exchange_ffn/pallas_call | solution.py:422
  1287.6 34.4 %combine.3 = bf16[8192,768]{1,0:T(8,128)(2,1)} custom-call(s32[256]{0:T(256)} %reshape_squeeze.36.reg_ref, s32[256]{0:T(256)} %reshape_squeeze.37.dst_ref, s32[256]{0:T(256)} %reshape_squeeze.38.cnt_ref, bf16[16384,768]{1,0:T(8,128)(2,1)} %bitcast.82, bf16[8192,768]{1,0:T(8,128)(2,1)} %get-tuple-element.23.h1_ref, f32[8192,1]{1,0:T(8,128)} %get-tuple-element.24.gate_ref, ...), custom_call_target="tpu_custom_call" | custom-call | flops 12884901888 | bytes 25165824 | tf_op jit(solution)/shard_map/combine/pallas_call | solution.py:219
  (70 shorter events, 13.7 us)
Async XLA Ops:
  6.5 641.8 %all-gather.11.cloned.1.call-start = ((), (), s32[]{:S(2)}) async-start(), calls=%async_computation.2 | async-start | bytes 42467328 | tf_op jit(solution)/shard_map/all_gather | solution.py:523
  11.4 636.9 %all-gather.13.cloned.1.call-start = ((), (), s32[]{:S(2)}) async-start(), calls=%async_computation.3 | async-start | bytes 42467328 | tf_op jit(solution)/shard_map/all_gather | solution.py:523
  16.3 0.9 copy-start.4
  16.3 1.2 copy-start.5
  16.3 7.0 copy-start.7
  16.4 995.0 %all-gather.7.cloned.1.call-start = ((), (), s32[]{:S(2)}) async-start(), calls=%async_computation | async-start | bytes 42467328 | tf_op jit(solution)/shard_map/all_gather | solution.py:523
  30.2 0.9 copy-start.11
  30.4 2.4 copy-start
  30.4 2.4 copy-start.1
  32.8 3.2 copy-start.2
  32.8 4.1 copy-start.3
  632.2 379.2 %all-gather.9.cloned.1.call-start = ((), (), s32[]{:S(2)}) async-start(), calls=%async_computation.1 | async-start | bytes 42467328 | tf_op jit(solution)/shard_map/all_gather | solution.py:523
  637.0 0.7 copy-start.8
  637.0 1.4 copy-start.9
  637.0 2.0 copy-start.10
  637.0 5.2 copy-start.6
  642.3 5.5 copy-start.12
Sparse Core Ops, SparseCore 0:
  11.6 175.2 all-gather.10
  188.5 323.7 all-gather.12
  632.3 172.3 all-gather.6
  806.2 171.0 all-gather.8

commit v3 on v2

--- a/solution.py
+++ b/solution.py
@@ -12,7 +12,7 @@
 NEG_BIG = -1e9
 CAP_FACTOR = 2
 TILE = 16
-PAIRS_PER_STEP = 1
+PAIRS_PER_STEP = 3
 SHARED = (1, 1)
 BF16 = jnp.bfloat16
 F32 = jnp.float32
@@ -262,8 +262,8 @@
         (packed_ref, up_ref, down_ref, ups_ref, downs_ref, ret_ref, recv_s, up_s, down_s, acc_s, w_sem, send_sem, recv_sem, back_sem,
          home_sem, x_h, up_h, down_h, in_sem, out_sem) = refs
     else:
-        (packed_ref, up_ref, down_ref, ret_ref, recv_s, up_s, down_s, acc_s, w_sem, send_sem, recv_sem, back_sem,
-         home_sem) = refs
+        (packed_ref, up_ref, down_ref, ret_ref, next_up_ref, next_down_ref, recv_s, up_s, down_s, acc_s, w_sem, send_sem, recv_sem,
+         back_sem, home_sem, next_up_s, next_down_s, next_sem) = refs
     cap, dim = packed_ref.shape[1], packed_ref.shape[2]
     inner = up_s.shape[2]
     halves = cap // block
@@ -306,6 +306,15 @@
 
     def home_out(n):
         return pltpu.make_async_copy(x_h.at[n % 2], ret_ref.at[(n // stay) * local + away + n % stay], out_sem.at[n % 2])
+
+    def share_in():
+        mine = pl.ds(away, local - away)
+        return (pltpu.make_async_copy(up_ref.at[layer + 1, mine], next_up_s, next_sem.at[0]),
+                pltpu.make_async_copy(down_ref.at[layer + 1, mine], next_down_s, next_sem.at[1]))
+
+    def share_out():
+        return (pltpu.make_async_copy(next_up_s, next_up_ref, next_sem.at[2]),
+                pltpu.make_async_copy(next_down_s, next_down_ref, next_sem.at[3]))
 
     barrier = pltpu.get_barrier_semaphore()
     for k in range(1, count):
@@ -321,12 +330,16 @@
     for j in range(away):
         for copy in weights(j):
             copy.start()
-    if stay:
-        for copy in home_in(0):
-            copy.start()
+    for copy in (home_in(0) if stay else share_in()):
+        copy.start()
     for j in range(away):
         for copy in weights(j):
             copy.wait()
+    if not stay:
+        for copy in share_in():
+            copy.wait()
+        for copy in share_out():
+            copy.start()
 
     def order(t):
         u = jnp.maximum(t - pieces, 0)
@@ -402,6 +415,9 @@
         own_out(p).wait()
     if stay:
         home_out(count * stay - 1).wait()
+    else:
+        for copy in share_out():
+            copy.wait()
 
 
 def exchange_ffn(packed, w_in, w_out, layer, count, away, ups=None, downs=None, block=256):
@@ -415,15 +431,20 @@
                pltpu.VMEM((away, inner, dim), BF16), pltpu.VMEM((block, dim), F32), dma((2, away)),
                dma((count, pieces)), dma((count, pieces)), dma((count, pieces)), dma((count, pieces))]
     operands = [packed, w_in, w_out]
-    if stay:
+    results = [jax.ShapeDtypeStruct(packed.shape, BF16)]
+    if not stay:
+        kept = local - away
+        results += [jax.ShapeDtypeStruct((kept, dim, inner), BF16), jax.ShapeDtypeStruct((kept, inner, dim), BF16)]
+        scratch += [pltpu.VMEM((kept, dim, inner), BF16), pltpu.VMEM((kept, inner, dim), BF16), dma((4,))]
+    else:
         scratch += [pltpu.VMEM((2, cap, dim), BF16), pltpu.VMEM((2, dim, inner), BF16), pltpu.VMEM((2, inner, dim), BF16),
                     dma((3, 2)), dma((2,))]
         operands += [ups, downs]
     return pl.pallas_call(
         functools.partial(exchange_kernel, layer=layer, count=count, local=local, away=away, block=block, stay=stay),
         in_specs=[pl.BlockSpec(memory_space=pl.ANY)] * len(operands),
-        out_specs=pl.BlockSpec(memory_space=pl.ANY),
-        out_shape=jax.ShapeDtypeStruct(packed.shape, BF16),
+        out_specs=[pl.BlockSpec(memory_space=pl.ANY)] * len(results),
+        out_shape=results,
         scratch_shapes=scratch,
         compiler_params=pltpu.CompilerParams(collective_id=layer, has_side_effects=True, vmem_limit_bytes=60 * 2**20),
         cost_estimate=pl.CostEstimate(flops=4 * count * (away + stay) * cap * dim * inner, bytes_accessed=nexp * cap * dim * 4,
@@ -514,33 +535,21 @@
         hidden = x_in.reshape(toks, model_dim)
         shared = [min(n, local - 1) for n in SHARED]
 
-        def gather(weight, layer, early, after):
-            if early is not None:
-                weight, _ = lax.optimization_barrier((weight, early))
-            own = weight[layer, local - shared[layer]:]
-            if after is not None:
-                own, _ = lax.optimization_barrier((own, after))
-            return lax.all_gather(own, 'ep', axis=0, tiled=True)
-
-        early = after = None
+        own = [w[0, local - shared[0]:] for w in (w_in, w_out)]
         for layer in range(layers):
             tables = [t[layer].reshape(num_seqs * nexp) for t in (reg, dst, tiles)]
-            if shared[layer]:
-                ups, downs = (gather(w, layer, early, after) for w in (w_in, w_out))
+            ups, downs = (lax.all_gather(w, 'ep', axis=0, tiled=True) for w in own)
             h1, b, gate = attention(hidden, mask_col, rel_bias, norm_scale[layer, 0][None], norm_scale[layer, 1][None],
                                     w_query[layer], w_key[layer], w_value[layer], w_attn_out[layer], wr[layer],
                                     expert_idx[layer].reshape(toks, 1), seq_len)
-            early = gate[:8]
             packed = pack(*tables, b, pos[layer].reshape(num_seqs, 1, seq_len), nexp, cap)
             packed = packed.reshape(nexp, cap, model_dim)
             away = local - shared[layer]
-            if shared[layer] and layer == layers - 1:
-                returned = exchange_ffn(packed, w_in, w_out, layer, count, away, ups, downs)
+            if layer == layers - 1:
+                returned, = exchange_ffn(packed, w_in, w_out, layer, count, away, ups, downs)
             else:
-                returned = exchange_ffn(packed, w_in, w_out, layer, count, away)
-                after = returned[0, :TILE, :128]
-                if shared[layer]:
-                    returned = home_ffn(fill[layer], packed, ups, downs, returned, local, away)
+                returned, *own = exchange_ffn(packed, w_in, w_out, layer, count, away)
+                returned = home_ffn(fill[layer], packed, ups, downs, returned, local, away)
             hidden = combine(*tables, returned.reshape(nexp * cap, model_dim), h1, gate, pos[layer].reshape(toks, 1), nexp, cap, seq_len)
         return hidden.reshape(num_seqs, seq_len, model_dim)
 

time: 1330 us -> 1290 us (0.970)
  Pallas kernels: 1260 us -> 1220 us
    pallas_call x2, Pallas kernels: 409 us -> 351 us  [attention(): pl.pallas_call(attention_kernel, grid=(nseq,), in_specs=[tok_spec, col_sp...]
    pallas_call x2, Pallas kernels: 621 us -> 649 us  [exchange_ffn(): pl.pallas_call(functools.partial(exchange_kernel, layer=layer, count=coun...]
  transfers between devices with their start and end apart: 4 -> 4, of which waited for: 0 -> 1; matrix products, arithmetic and copies ran while one was open for 4% -> 3% of each run, Pallas kernels for 71% -> 71%
where the time goes in v3:
time: 1290 us
  Pallas kernels  1220 us (95%)
  local copies, waits for them, and re-layouts  40.8 us (3%)
  between operations  13.4 us (1%)
    pallas_call x2, Pallas kernels, exchange_ffn(): pl.pallas_call(functools.partial(exchange_kernel, layer=layer, count=coun...  649 us
    pallas_call x2, Pallas kernels, attention(): pl.pallas_call(attention_kernel, grid=(nseq,), in_specs=[tok_spec, col_sp...  351 us
    pallas_call x1, Pallas kernels, home_ffn(): pl.pallas_call(functools.partial(home_kernel, local=local, away=away, blo...  80.1 us
    pallas_call x2, Pallas kernels, pack(): pl.pallas_call(functools.partial(pack_kernel, nexp=nexp, cap=cap), grid_s...  75.7 us
    pallas_call x2, Pallas kernels, combine(): pl.pallas_call(functools.partial(combine_kernel, nexp=nexp, cap=cap), gri...  68.8 us
  transfers between devices with their start and end apart: 4, of which 1 were waited for; matrix products, arithmetic and copies ran while one was open for 3% of the time, Pallas kernels for 71%

profile of v3, /device:TPU:113, one launch (start us, length us, event | category | flops | bytes accessed | tf_op | source)
XLA Modules:
  0.0 1289.0 jit_solution(12780272601769324960)
XLA Ops:
  6.6 4.8 slice.99
  11.5 4.8 slice.100
  16.5 0.8 copy-done.4
  23.4 2.9 copy.73
  27.3 2.8 copy.75
  31.0 0.7 fusion
  32.4 0.7 fusion.16
  33.1 1.1 slice_bitcast_fusion.8
  34.3 2.5 slice_bitcast_fusion.2
  37.4 0.9 copy-done.3
  38.3 2.3 slice_bitcast_fusion
  40.6 175.5 %attention.2 = (bf16[8192,768]{1,0:T(8,128)(2,1)}, bf16[8192,768]{1,0:T(8,128)(2,1)}, f32[8192,1]{1,0:T(8,128)}) custom-call(bf16[8192,768]{1,0:T(8,128)(2,1)} %bitcast.89, s32[8192,1]{1,0:T(8,128)} %bitcast.79, f32[12,512,512]{2,1,0:T(8,128)} %bias_ref.3, f32[1,768]{1,0:T(1,128)} %get-tuple-element.59.g0_ref, f32[1,768]{1,0:T(1,128)} %get-tuple-element.58.g1_ref, ...), custom_call_target="tpu_custom_call" | custom-call | flops 51539607552 | bytes 37748736 | tf_op jit(solution)/shard_map/attention/pallas_call | solution.py:111
  216.1 37.6 %pack.2 = bf16[16384,768]{1,0:T(8,128)(2,1)} custom-call(s32[256]{0:T(256)} %reshape_squeeze.39.reg_ref, s32[256]{0:T(256)} %reshape_squeeze.40.dst_ref, s32[256]{0:T(256)} %reshape_squeeze.41.cnt_ref, bf16[8192,768]{1,0:T(8,128)(2,1)} %get-tuple-element.14.b_ref, s32[16,1,512]{2,1,0:T(1,128)} %get-tuple-element.65.pos_ref), custom_call_target="tpu_custom_call" | custom-call | flops 12884901888 | bytes 25165824 | tf_op jit(solution)/shard_map/pack/pallas_call | solution.py:172
  253.7 373.6 %exchange_ffn.2 = (bf16[16,1024,768]{2,1,0:T(8,128)(2,1)}, bf16[1,768,3072]{2,1,0:T(8,128)(2,1)}, bf16[1,3072,768]{2,1,0:T(8,128)(2,1)}) custom-call(bf16[16,1024,768]{2,1,0:T(8,128)(2,1)} %bitcast.77, bf16[2,2,768,3072]{3,2,1,0:T(8,128)(2,1)} %refs_1_.3, bf16[2,2,3072,768]{3,2,1,0:T(8,128)(2,1)} %refs_2_.3), custom_call_target="tpu_custom_call" | custom-call | flops 77309411328 | bytes 50331648 | tf_op jit(solution)/shard_map/exchange_ffn/pallas_call | solution.py:443
  630.1 2.6 copy.64.pos_ref
  632.8 2.7 copy.77
  635.4 2.8 copy.68.pos_ref
  638.7 80.1 %home_ffn.1 = bf16[16,1024,768]{2,1,0:T(8,128)(2,1)} custom-call(s32[16]{0:T(128)} %slice_bitcast_fusion.16.fill_ref, bf16[16,1024,768]{2,1,0:T(8,128)(2,1)} %bitcast.78, bf16[8,768,3072]{2,1,0:T(8,128)(2,1)} %bitcast.74, bf16[8,3072,768]{2,1,0:T(8,128)(2,1)} %bitcast.75, ...), custom_call_target="tpu_custom_call", output_to_operand_aliasing={{}: (4, {})} | custom-call | flops 38654705664 | bytes 25165824 | tf_op jit(solution)/shard_map/home_ffn/pallas_call | solution.py:473
  718.8 34.5 %combine.2.x_ref = bf16[8192,768]{1,0:T(8,128)(2,1)} custom-call(s32[256]{0:T(256)} %reshape_squeeze.39.reg_ref, s32[256]{0:T(256)} %reshape_squeeze.40.dst_ref, s32[256]{0:T(256)} %reshape_squeeze.41.cnt_ref, bf16[16384,768]{1,0:T(8,128)(2,1)} %bitcast.73, bf16[8192,768]{1,0:T(8,128)(2,1)} %get-tuple-element.16.h1_ref, ...), custom_call_target="tpu_custom_call" | custom-call | flops 12884901888 | bytes 25165824 | tf_op jit(solution)/shard_map/combine/pallas_call | solution.py:219
  753.3 175.5 %attention.3 = (bf16[8192,768]{1,0:T(8,128)(2,1)}, bf16[8192,768]{1,0:T(8,128)(2,1)}, f32[8192,1]{1,0:T(8,128)}) custom-call(bf16[8192,768]{1,0:T(8,128)(2,1)} %combine.2.x_ref, s32[8192,1]{1,0:T(8,128)} %bitcast.80, f32[12,512,512]{2,1,0:T(8,128)} %bias_ref.3, f32[1,768]{1,0:T(1,128)} %get-tuple-element.60.g0_ref, f32[1,768]{1,0:T(1,128)} %get-tuple-element.57.g1_ref, ...), custom_call_target="tpu_custom_call" | custom-call | flops 51539607552 | bytes 37748736 | tf_op jit(solution)/shard_map/attention/pallas_call | solution.py:111
  928.8 38.1 %pack.3 = bf16[16384,768]{1,0:T(8,128)(2,1)} custom-call(s32[256]{0:T(256)} %reshape_squeeze.36.reg_ref, s32[256]{0:T(256)} %reshape_squeeze.37.dst_ref, s32[256]{0:T(256)} %reshape_squeeze.38.cnt_ref, bf16[8192,768]{1,0:T(8,128)(2,1)} %get-tuple-element.18.b_ref, s32[16,1,512]{2,1,0:T(1,128)} %get-tuple-element.46.pos_ref), custom_call_target="tpu_custom_call" | custom-call | flops 12884901888 | bytes 25165824 | tf_op jit(solution)/shard_map/pack/pallas_call | solution.py:172
  966.9 5.4 all-gather.9.cloned.1.call-done.refs_4_
  972.3 275.8 %exchange_ffn.3 = bf16[16,1024,768]{2,1,0:T(8,128)(2,1)} custom-call(bf16[16,1024,768]{2,1,0:T(8,128)(2,1)} %bitcast.90, bf16[2,2,768,3072]{3,2,1,0:T(8,128)(2,1)} %refs_1_.3, bf16[2,2,3072,768]{3,2,1,0:T(8,128)(2,1)} %refs_2_.3, bf16[8,768,3072]{2,1,0:T(8,128)(2,1)} %all-gather.7.cloned.1.call-done.refs_3_, ...), custom_call_target="tpu_custom_call" | custom-call | flops 154618822656 | bytes 50331648 | tf_op jit(solution)/shard_map/exchange_ffn/pallas_call | solution.py:443
  1248.1 34.4 %combine.3 = bf16[8192,768]{1,0:T(8,128)(2,1)} custom-call(s32[256]{0:T(256)} %reshape_squeeze.36.reg_ref, s32[256]{0:T(256)} %reshape_squeeze.37.dst_ref, s32[256]{0:T(256)} %reshape_squeeze.38.cnt_ref, bf16[16384,768]{1,0:T(8,128)(2,1)} %bitcast.76, bf16[8192,768]{1,0:T(8,128)(2,1)} %get-tuple-element.21.h1_ref, f32[8192,1]{1,0:T(8,128)} %get-tuple-element.22.gate_ref, ...), custom_call_target="tpu_custom_call" | custom-call | flops 12884901888 | bytes 25165824 | tf_op jit(solution)/shard_map/combine/pallas_call | solution.py:219
  (72 shorter events, 12.9 us)
Async XLA Ops:
  6.5 632.2 %all-gather.11.cloned.1.call-start = ((), (), s32[]{:S(2)}) async-start(), calls=%async_computation.2 | async-start | bytes 42467328 | tf_op jit(solution)/shard_map/all_gather | solution.py:541
  11.5 627.3 %all-gather.13.cloned.1.call-start = ((), (), s32[]{:S(2)}) async-start(), calls=%async_computation.3 | async-start | bytes 42467328 | tf_op jit(solution)/shard_map/all_gather | solution.py:541
  16.3 0.9 copy-start.4
  16.3 1.2 copy-start.5
  16.3 7.0 copy-start.9
  16.4 950.5 %all-gather.7.cloned.1.call-start = ((), (), s32[]{:S(2)}) async-start(), calls=%async_computation | async-start | bytes 42467328 | tf_op jit(solution)/shard_map/all_gather | solution.py:541
  30.9 0.9 copy-start.13
  31.0 3.2 copy-start
  31.0 3.2 copy-start.1
  34.3 3.2 copy-start.2
  34.3 4.1 copy-start.3
  627.4 344.9 %all-gather.9.cloned.1.call-start = ((), (), s32[]{:S(2)}) async-start(), calls=%async_computation.1 | async-start | bytes 42467328 | tf_op jit(solution)/shard_map/all_gather | solution.py:541
  627.4 0.7 copy-start.10
  627.5 1.4 copy-start.11
  627.5 2.0 copy-start.12
  627.5 2.6 copy-start.7
  628.0 4.7 copy-start.8
  632.7 2.7 copy-start.6
  635.4 2.8 copy-start.14
Sparse Core Ops, SparseCore 0:
  11.6 175.2 all-gather.10
  188.5 369.6 all-gather.12
  627.5 172.2 all-gather.6
  801.2 171.0 all-gather.8
